TPU v7x, 128 devices: a whole 4x4x4 slice. The times are simulated.
128 devices in a mesh: dom: 128 (over y, z, x, core).
Axes of the slice: x: 4, y: 4, z: 4, core: 2. Of those that a mesh axis runs over, the one named last changes fastest.
Arguments:
- right_side: float32 [131072, 3], P('dom'), may hold values from -10 to 10
- fine_diagonal: float32 [131072, 3], P('dom'), may hold values from 2 to 4
- fine_columns: int32 [131072, 27], P('dom'), may hold values from 0 to 131071, as said below
- fine_blocks: float32 [131072, 27, 3, 3], P('dom'), may hold values from -0.625 to 0.625
- aggregate_of_node: int32 [131072], P('dom'), may hold values from 0 to 31, as said below
- coarse_row_of_aggregate: int32 [4096], P('dom'), may hold values from 0 to 4095, as said below
- coarse_diagonal: float32 [4096, 3], P('dom'), may hold values from 2 to 4
- coarse_columns: int32 [4096, 27], P('dom'), may hold values from 0 to 4095
- coarse_blocks: float32 [4096, 27, 3, 3], P('dom'), may hold values from -0.625 to 0.625
Outputs:
- solution: float32 [131072, 3], P('dom')
- correction: float32 [4096, 3], P('dom')
Inputs may be any that keep to these rules, and one draw needn't show every extreme that they name: Every entry of fine_columns differs from its row number by at most 256, and some entry by exactly 256. `aggregate_of_node`: on each device every aggregate number 0 to 31 is used by at least one of its nodes. coarse_row_of_aggregate is a permutation of 0 to 4095; among the 32 aggregates of one device (an aligned block of entries) at most 8 get rows of any one owner, and exactly 8 for some owner.
All inputs are finite; a program needn't handle non-finite values.
Results may differ from a plain program's by a relative error of at most 0.0003.
Values sent between devices are 32-bit elements.
A program may use at most 64 MiB of HBM per device.

v0:
```python
import jax
import jax.numpy as jnp
from jax import lax
from jax.sharding import Mesh
from jax.sharding import PartitionSpec as P

CAP = 8
WIN = 256
SWEEPS = 2
CSWEEPS = 6
DOM = ("dom_0", "dom_1", "dom_2", "dom_3")


damping = 0.7
highest = lax.Precision.HIGHEST


def padded_2(value, sides, width, wrap):
    for axis, dim in sides:
        peers, length = lax.axis_size(axis), value.shape[dim]
        up = [(i, (i + 1) % peers) for i in range(peers if wrap else peers - 1)]
        down = [(j, i) for i, j in up]
        last = lax.slice_in_dim(value, length - width, length, axis=dim)
        initial = lax.slice_in_dim(value, 0, width, axis=dim)
        before = lax.ppermute(last, axis, up)
        after = lax.ppermute(initial, axis, down)
        value = jnp.concatenate([before, value, after], axis=dim)
    return value


def split_up(value, dim, peers):
    return jnp.stack(jnp.split(value, peers, axis=dim))


def joined_along(tiles, dim):
    tiles = jnp.moveaxis(tiles, 0, dim)
    shape = tiles.shape
    return tiles.reshape(*shape[:dim], shape[dim] * shape[dim + 1], *shape[dim + 2 :])


def turned_blocks(tiles, axes, sequence):
    inside = tiles.shape[1:]
    whole = tiles.reshape(*(lax.axis_size(a) for a in axes), *inside)
    for k in sequence:
        whole = lax.all_to_all(whole, axes[k], k, k, tiled=True)
    return whole.reshape(-1, *inside)


def exchange_by_chip(value, groups, sequence, split_dim, concat_dim):
    peers = lax.axis_size(groups[0]) * lax.axis_size(groups[1])
    tiles = split_up(value, split_dim, peers)
    return joined_along(turned_blocks(tiles, groups, sequence), concat_dim)


def couple(blocks, nearby):
    return jnp.sum(blocks * nearby[:, :, None, :], axis=(1, 3))


def apply_fine(field, fine_diagonal, fine_columns, fine_blocks):
    row_count = fine_columns.shape[0]
    padded = padded_2(field, ((DOM, 0),), WIN, False)
    first_row = lax.axis_index(DOM) * row_count - WIN
    local_columns = (fine_columns - first_row).astype(jnp.int32)
    nearby = padded[local_columns]
    return fine_diagonal * field - couple(fine_blocks, nearby)


def apply_coarse(field, coarse_diagonal, coarse_columns, coarse_blocks):
    gathered = lax.all_gather(field, DOM, axis=0, tiled=True)
    nearby = gathered[coarse_columns]
    return coarse_diagonal * field - couple(coarse_blocks, nearby)


def body(
    right_side,
    fine_diagonal,
    fine_columns,
    fine_blocks,
    aggregate_of_node,
    coarse_row_of_aggregate,
    coarse_diagonal,
    coarse_columns,
    coarse_blocks,
):
    solution = damping * right_side / fine_diagonal
    for sweep in range(SWEEPS - 1):
        solution = (
            solution
            + damping
            * (right_side - apply_fine(solution, fine_diagonal, fine_columns, fine_blocks))
            / fine_diagonal
        )
    residual = right_side - apply_fine(solution, fine_diagonal, fine_columns, fine_blocks)
    aggregate_count = coarse_diagonal.shape[0]
    devices = lax.axis_size(DOM)
    aggregate_ids = jnp.arange(aggregate_count, dtype=jnp.int32)
    sums_here = jax.ops.segment_sum(residual, aggregate_of_node, num_segments=aggregate_count)
    owners = coarse_row_of_aggregate // aggregate_count
    member = (owners[:, None] == jnp.arange(devices, dtype=jnp.int32)[None, :]).astype(jnp.float32)
    earlier = (aggregate_ids[None, :] < aggregate_ids[:, None]).astype(jnp.float32)
    before = jnp.dot(earlier, member, precision=highest)
    position = jnp.sum(before * member, axis=1).astype(jnp.int32)
    bucket = (owners * CAP + position).astype(jnp.int32)
    local_rows = (coarse_row_of_aggregate - owners * aggregate_count).astype(jnp.int32)
    slot_out = jnp.full((devices * CAP,), aggregate_count, jnp.int32).at[bucket].set(local_rows)
    slot_in = exchange_by_chip(slot_out, (("dom_0", "dom_1", "dom_2"), "dom_3"), (0, 1), 0, 0)
    outgoing = jnp.zeros((devices * CAP, 3), jnp.float32).at[bucket].set(sums_here)
    arrived = exchange_by_chip(outgoing, (("dom_0", "dom_1", "dom_2"), "dom_3"), (0, 1), 0, 0)
    coarse_rhs = jnp.zeros((aggregate_count, 3), jnp.float32).at[slot_in].add(arrived, mode="drop")
    correction = damping * coarse_rhs / coarse_diagonal
    for sweep in range(CSWEEPS - 1):
        correction = (
            correction
            + damping
            * (
                coarse_rhs
                - apply_coarse(correction, coarse_diagonal, coarse_columns, coarse_blocks)
            )
            / coarse_diagonal
        )
    sending = jnp.take(correction, slot_in, axis=0, mode="fill", fill_value=0.0)
    returned = exchange_by_chip(sending, (("dom_0", "dom_1", "dom_2"), "dom_3"), (0, 1), 0, 0)
    label_values = returned[bucket]
    solution = solution + label_values[aggregate_of_node]
    for sweep in range(SWEEPS):
        solution = (
            solution
            + damping
            * (right_side - apply_fine(solution, fine_diagonal, fine_columns, fine_blocks))
            / fine_diagonal
        )
    return (solution, correction)


def solution(mesh):
    torus = Mesh(mesh.devices.reshape(4, 4, 4, 2), ("dom_0", "dom_1", "dom_2", "dom_3"))
    return jax.shard_map(
        body,
        mesh=torus,
        in_specs=(
            P(DOM, None),
            P(DOM, None),
            P(DOM, None),
            P(DOM, None, None, None),
            P(DOM),
            P(DOM),
            P(DOM, None),
            P(DOM, None),
            P(DOM, None, None, None),
        ),
        out_specs=(P(DOM, None), P(DOM, None)),
        check_vma=False,
    )
```

profile of v0, /device:TPU:1, one launch (start us, length us, event | category | flops | bytes accessed | tf_op | source)
XLA Modules:
  0.0 756.7 jit_solution(1142505852747501974)
XLA Ops:
  1.4 4.5 collective-permute-start
  10.1 9.7 %stack.1289 = s32[128,8]{1,0:T(8,128)} concatenate(s32[1,8]{1,0:T(1,128)S(1)} %get-tuple-element.405, s32[1,8]{1,0:T(1,128)S(1)} %get-tuple-element.404, s32[1,8]{1,0:T(1,128)S(1)} %get-tuple-element.403, s32[1,8]{1,0:T(1,128)S(1)} %get-tuple-element.402, s32[1,8]{1,0:T(1,128)S(1)} %get-tuple-element.401, s32[1,8]{1,0:T(1,128)S(1)} %get-tuple-element.400, ...), dimensions={0} | concatenate | bytes 8192 | tf_op jit(solution)/shard_map/stack | solution.py:32
  19.8 10.8 %all-to-all-start = ((s32[64,2,8]{2,1,0:T(2,128)}), s32[64,2,8]{2,1,0:T(2,128)S(1)}, u32[]{:S(2)}, u32[]{:S(2)}) async-start(s32[64,2,8]{2,1,0:T(2,128)} %bitcast.128), calls=%async_computation | async-start | bytes 131072 | tf_op jit(solution)/shard_map/all_to_all | solution.py:45
  32.7 91.5 %gather_fusion = f32[27648,3]{1,0:T(8,128)} fusion(f32[1536,3]{1,0:T(8,128)S(1)} %copy.2716, s32[27648]{0:T(1024)S(1)} %broadcast_clamp_fusion), kind=kCustom, calls=%fused_computation | custom fusion | bytes 774144 | tf_op jit(solution)/shard_map/gather | solution.py:64
  124.2 8.3 %copy.2717 = f32[27648,3]{0,1:T(4,128)S(1)} copy(f32[27648,3]{1,0:T(8,128)} %gather_fusion) | data formatting | bytes 663552 | tf_op jit(solution)/shard_map/gather | solution.py:64
  132.5 3.0 reshape.61
  137.7 4.3 collective-permute-start.2
  144.1 3.4 all_to_all.30
  149.4 91.5 %gather_fusion.1 = f32[27648,3]{1,0:T(8,128)} fusion(f32[1536,3]{1,0:T(8,128)S(1)} %copy.2722, s32[27648]{0:T(1024)S(1)} %broadcast_clamp_fusion), kind=kCustom, calls=%fused_computation.1 | custom fusion | bytes 774144 | tf_op jit(solution)/shard_map/gather | solution.py:64
  240.9 8.3 %copy.2723 = f32[27648,3]{0,1:T(4,128)S(1)} copy(f32[27648,3]{1,0:T(8,128)} %gather_fusion.1) | data formatting | bytes 663552 | tf_op jit(solution)/shard_map/gather | solution.py:64
  249.2 3.0 reshape.69
  254.5 6.0 scatter_custom_fusion.1
  274.4 11.1 %all-to-all-start.2 = ((f32[64,2,8,3]{2,1,3,0:T(2,128)}), f32[64,2,8,3]{2,1,3,0:T(2,128)S(1)}, u32[]{:S(2)}, u32[]{:S(2)}) async-start(f32[64,2,8,3]{2,1,3,0:T(2,128)} %copy.2855), calls=%async_computation.2 | async-start | bytes 393216 | tf_op jit(solution)/shard_map/all_to_all | solution.py:45
  285.5 9.7 %all-to-all-done.2 = f32[64,2,8,3]{2,1,3,0:T(2,128)S(1)} async-done(((f32[64,2,8,3]{2,1,3,0:T(2,128)}), f32[64,2,8,3]{2,1,3,0:T(2,128)S(1)}, u32[]{:S(2)}, u32[]{:S(2)}) %all-to-all-start.2) | async-done | bytes 12320 | tf_op jit(solution)/shard_map/all_to_all | solution.py:45
  295.4 4.6 all_to_all.31
  301.6 6.0 scatter_custom_fusion.3
  307.7 33.6 %all-gather = f32[128,32,3]{1,2,0:T(4,128)S(1)} all-gather(f32[1,32,3]{1,2,0:T(4,128)S(1)} %fusion.11), channel_id=1, replica_groups=mesh['dom_0'=4,'dom_1'=4,'dom_2'=4,'dom_3'=2] {'dom_0','dom_1','dom_2','..., dimensions={0}, use_global_device_ids=true | all-gather | bytes 49536 | tf_op jit(solution)/shard_map/all_gather | solution.py:69
  344.4 33.4 %all-gather.1 = f32[128,32,3]{1,2,0:T(4,128)S(1)} all-gather(f32[1,32,3]{1,2,0:T(4,128)S(1)} %bitcast.827), channel_id=1, replica_groups=mesh['dom_0'=4,'dom_1'=4,'dom_2'=4,'dom_3'=2] {'dom_0','dom_1','dom_2','..., dimensions={0}, use_global_device_ids=true | all-gather | bytes 49536 | tf_op jit(solution)/shard_map/all_gather | solution.py:69
  380.9 33.4 %all-gather.2 = f32[128,32,3]{1,2,0:T(4,128)S(1)} all-gather(f32[1,32,3]{1,2,0:T(4,128)S(1)} %bitcast.825), channel_id=1, replica_groups=mesh['dom_0'=4,'dom_1'=4,'dom_2'=4,'dom_3'=2] {'dom_0','dom_1','dom_2','..., dimensions={0}, use_global_device_ids=true | all-gather | bytes 49536 | tf_op jit(solution)/shard_map/all_gather | solution.py:69
  417.4 33.6 %all-gather.3 = f32[128,32,3]{1,2,0:T(4,128)S(1)} all-gather(f32[1,32,3]{1,2,0:T(4,128)S(1)} %bitcast.826), channel_id=1, replica_groups=mesh['dom_0'=4,'dom_1'=4,'dom_2'=4,'dom_3'=2] {'dom_0','dom_1','dom_2','..., dimensions={0}, use_global_device_ids=true | all-gather | bytes 49536 | tf_op jit(solution)/shard_map/all_gather | solution.py:69
  454.2 33.4 %all-gather.4 = f32[128,32,3]{1,2,0:T(4,128)S(1)} all-gather(f32[1,32,3]{1,2,0:T(4,128)S(1)} %bitcast.824), channel_id=1, replica_groups=mesh['dom_0'=4,'dom_1'=4,'dom_2'=4,'dom_3'=2] {'dom_0','dom_1','dom_2','..., dimensions={0}, use_global_device_ids=true | all-gather | bytes 49536 | tf_op jit(solution)/shard_map/all_gather | solution.py:69
  506.7 5.6 all-to-all-start.4
  512.3 9.5 %all-to-all-done.4 = f32[64,2,8,3]{2,1,3,0:T(2,128)S(1)} async-done(((f32[64,2,8,3]{2,1,3,0:T(2,128)}), f32[64,2,8,3]{2,1,3,0:T(2,128)S(1)}, u32[]{:S(2)}, u32[]{:S(2)}) %all-to-all-start.4) | async-done | bytes 12320 | tf_op jit(solution)/shard_map/all_to_all | solution.py:45
  522.0 4.7 all_to_all.32
  528.4 2.8 gather_fusion.9
  535.8 3.0 collective-permute-done.5
  539.1 91.5 %gather_fusion.10 = f32[27648,3]{1,0:T(8,128)} fusion(f32[1536,3]{1,0:T(8,128)S(1)} %copy.3009, s32[27648]{0:T(1024)S(1)} %broadcast_clamp_fusion), kind=kCustom, calls=%fused_computation.10 | custom fusion | bytes 774144 | tf_op jit(solution)/shard_map/gather | solution.py:64
  630.6 8.3 %copy.3010 = f32[27648,3]{0,1:T(4,128)S(1)} copy(f32[27648,3]{1,0:T(8,128)} %gather_fusion.10) | data formatting | bytes 663552 | tf_op jit(solution)/shard_map/gather | solution.py:64
  638.9 3.0 reshape.141
  651.2 91.5 %gather_fusion.11 = f32[27648,3]{1,0:T(8,128)} fusion(f32[1536,3]{1,0:T(8,128)S(1)} %copy.3012, s32[27648]{0:T(1024)S(1)} %broadcast_clamp_fusion), kind=kCustom, calls=%fused_computation.11 | custom fusion | bytes 774144 | tf_op jit(solution)/shard_map/gather | solution.py:64
  742.7 8.3 %copy.3013 = f32[27648,3]{0,1:T(4,128)S(1)} copy(f32[27648,3]{1,0:T(8,128)} %gather_fusion.11) | data formatting | bytes 663552 | tf_op jit(solution)/shard_map/gather | solution.py:64
  751.0 3.0 reshape.149
  (666 shorter events, 80.2 us)
Async XLA Ops:
  0.6 31.6 %copy-start.6 = (s32[32,27]{1,0:T(8,128)S(1)}, s32[32,27]{1,0:T(8,128)}, u32[]{:S(2)}) copy-start(s32[32,27]{1,0:T(8,128)} %param.16) | copy-start | bytes 10372
  1.4 31.0 %collective-permute-start = (f32[256,3]{0,1:T(4,128)S(1)}, f32[256,3]{0,1:T(4,128)S(1)}, u32[]{:S(2)}, u32[]{:S(2)}) collective-permute-start(f32[256,3]{0,1:T(4,128)S(1)} %get-tuple-element.276), channel_id=1, source_target_pairs={{0,1},{1,2},{2,3},{3,4},{4,5},{5,6},{6,7},{7,8},{8,9},{9,10},{10,1... | collective-permute-start | bytes 9224 | tf_op jit(solution)/shard_map/ppermute | solution.py:25
  5.9 26.5 %collective-permute-start.1 = (f32[256,3]{0,1:T(4,128)S(1)}, f32[256,3]{0,1:T(4,128)S(1)}, u32[]{:S(2)}, u32[]{:S(2)}) collective-permute-start(f32[256,3]{0,1:T(4,128)S(1)} %get-tuple-element.277), channel_id=1, source_target_pairs={{1,0},{2,1},{3,2},{4,3},{5,4},{6,5},{7,6},{8,7},{9,8},{10,9},{11,1... | collective-permute-start | bytes 9224 | tf_op jit(solution)/shard_map/ppermute | solution.py:26
  19.8 124.0 %all-to-all-start = ((s32[64,2,8]{2,1,0:T(2,128)}), s32[64,2,8]{2,1,0:T(2,128)S(1)}, u32[]{:S(2)}, u32[]{:S(2)}) async-start(s32[64,2,8]{2,1,0:T(2,128)} %bitcast.128), calls=%async_computation | async-start | bytes 131072 | tf_op jit(solution)/shard_map/all_to_all | solution.py:45
  132.5 4.9 copy-start
  135.5 2.1 copy-start.3
  135.5 2.1 copy-start.4
  137.7 11.4 %collective-permute-start.2 = (f32[256,3]{0,1:T(4,128)S(1)}, f32[256,3]{0,1:T(4,128)S(1)}, u32[]{:S(2)}, u32[]{:S(2)}) collective-permute-start(f32[256,3]{0,1:T(4,128)S(1)} %get-tuple-element.274), channel_id=1, source_target_pairs={{0,1},{1,2},{2,3},{3,4},{4,5},{5,6},{6,7},{7,8},{8,9},{9,10},{10,1... | collective-permute-start | bytes 9224 | tf_op jit(solution)/shard_map/ppermute | solution.py:25
  142.0 7.1 collective-permute-start.3
  252.2 2.3 copy-start.8
  261.6 46.1 %copy-start.5 = (f32[32,3]{0,1:T(4,128)S(1)}, f32[32,3]{0,1:T(4,128)}, u32[]{:S(2)}) copy-start(f32[32,3]{0,1:T(4,128)} %param.15) | copy-start | bytes 1156
  274.4 20.8 %all-to-all-start.2 = ((f32[64,2,8,3]{2,1,3,0:T(2,128)}), f32[64,2,8,3]{2,1,3,0:T(2,128)S(1)}, u32[]{:S(2)}, u32[]{:S(2)}) async-start(f32[64,2,8,3]{2,1,3,0:T(2,128)} %copy.2855), calls=%async_computation.2 | async-start | bytes 393216 | tf_op jit(solution)/shard_map/all_to_all | solution.py:45
  342.1 2.2 copy-start.2
  490.7 2.9 copy-start.7
  506.7 15.2 %all-to-all-start.4 = ((f32[64,2,8,3]{2,1,3,0:T(2,128)}), f32[64,2,8,3]{2,1,3,0:T(2,128)S(1)}, u32[]{:S(2)}, u32[]{:S(2)}) async-start(f32[64,2,8,3]{2,1,3,0:T(2,128)} %copy.3005), calls=%async_computation.4 | async-start | bytes 393216 | tf_op jit(solution)/shard_map/all_to_all | solution.py:45
  531.4 4.4 collective-permute-start.4
  533.9 4.9 collective-permute-start.5
  638.9 4.9 copy-start.1
  644.0 4.6 collective-permute-start.6
  646.0 4.9 collective-permute-start.7
where the time goes:
time: 764 us; the launch traced here: 757 us
  local copies, waits for them, and re-layouts  482 us (63%)
  blocking collectives  180 us (24%)
  starting transfers between devices  49.1 us (6%)
  waiting for transfers between devices  24.5 us (3%)
  other arithmetic  18.7 us (2%)
    gather x16, local copies, waits for them, and re-layouts, apply_fine(): nearby = padded[local_columns]  419 us
    all_gather x5, blocking collectives, apply_coarse(): gathered = lax.all_gather(field, DOM, axis=0, tiled=True)  167 us
    all_to_all x3, starting transfers between devices, turned_blocks(): whole = lax.all_to_all(whole, axes[k], k, k, tiled=True)  27.6 us
    split x270, local copies, waits for them, and re-layouts, split_up(): return jnp.stack(jnp.split(value, peers, axis=dim))  20.8 us
    all_to_all x3, waiting for transfers between devices, turned_blocks(): whole = lax.all_to_all(whole, axes[k], k, k, tiled=True)  19.2 us
  transfers between devices with their start and end apart: 11, of which 4 were waited for; matrix products, arithmetic and copies ran while one was open for 16% of the time, Pallas kernels for 0%

commit v1 on v0

v1 whole, which is shorter than its diff:
```python
import jax
import jax.numpy as jnp
from jax import lax
from jax.experimental import pallas as pl
from jax.experimental.pallas import tpu as pltpu
from jax.sharding import PartitionSpec as P

DEVICES = 128
NODE_DEV = 1024
WIN = 256
NNZ = 27
AGG_DEV = 32
CSWEEPS = 6
LANES = 128
BLOCKS = NODE_DEV // LANES
SIDE = WIN // LANES
REACH = 2 * SIDE + 1
CUBE = 16
GROUPS = 8
CROWS = 32
DAMP = 0.7
KEEP = 1.0 - DAMP
CUBE_BITS = (0, 1, 3, 5)
GROUP_BITS = (2, 4, 6)
MESH = pl.DeviceIdType.MESH
F32, I32, BF16 = jnp.float32, jnp.int32, jnp.bfloat16


def position_of(row):
    def bit(p):
        return (row >> p) & 1

    high = bit(10) * 16 + bit(8) * 8 + bit(6) * 4 + bit(5) * 2 + bit(11)
    lane = bit(9) * 64 + bit(7) * 32 + (row & 31)
    return high * LANES + lane


def spread(row):
    return jnp.broadcast_to(row, (8, LANES))


def pick(row, lane):
    return jnp.take_along_axis(spread(row), lane, axis=1, mode="promise_in_bounds")


def gather_rows(place, rows, count):
    high, lane = place >> 7, place & 127
    values = [None] * 3
    for r in range(count):
        hit = high == r
        for c in range(3):
            taken = pick(rows(r, c), lane)
            values[c] = taken if r == 0 else jnp.where(hit, taken, values[c])
    return values


def kernel(
    b_h, d_h, q_h, a_h, agg_h, row_h, cd_h, cq_h, ca_h,
    sol_o, cor_o,
    b_v, d_v, q_v, a_v, agg_v, row_v, cd_v, cq_v, ca_v,
    w_v, s1_v, q_s, y_v, r_v, onehot, idx_v,
    f1, hl1, hr1, f2, hl2, hr2, f3, f4, hl4, hr4,
    stage, e0a, e0b, s1a, s1b,
    pack, rm, mx, mp,
    inv_v, dt_v, cbuf,
    load_sem, halo_send, halo_recv, far_send, far_recv, sweep_send, sweep_recv,
):
    me = lax.axis_index("dom")

    def bit(p):
        return (me // (1 << p)) % 2

    member = bit(5) * 8 + bit(3) * 4 + bit(1) * 2 + bit(0)
    group = bit(6) * 4 + bit(4) * 2 + bit(2)
    group_low, group_high = bit(4) * 2 + bit(2), bit(6)

    def flipped(bits, k):
        other = me
        for n, p in enumerate(bits):
            if (k >> n) & 1:
                other = other + (1 - 2 * bit(p)) * (1 << p)
        return other

    cube_peers = [flipped(CUBE_BITS, k) for k in range(1, CUBE)]
    group_peers = [flipped(GROUP_BITS, k) for k in range(1, GROUPS)]
    left, right = (me + DEVICES - 1) % DEVICES, (me + 1) % DEVICES

    loads = []
    for n, (src, dst) in enumerate(
        (
            (b_h, b_v), (d_h, d_v), (agg_h, agg_v), (row_h, row_v), (cd_h, cd_v),
            (cq_h, cq_v), (ca_h, ca_v), (q_h, q_v), (a_h, a_v),
        )
    ):
        copy = pltpu.make_async_copy(src, dst, load_sem.at[n])
        copy.start()
        loads.append(copy)

    barrier = pltpu.get_barrier_semaphore()
    for peer in cube_peers + group_peers + [left, right]:
        pl.semaphore_signal(barrier, inc=1, device_id=(peer,), device_id_type=MESH)

    def send(src, dst, send_sem, recv_sem, peer):
        pltpu.make_async_remote_copy(
            src_ref=src, dst_ref=dst, send_sem=send_sem, recv_sem=recv_sem,
            device_id=(peer,), device_id_type=MESH,
        ).start()

    def wait_bytes(ref, sem):
        pltpu.make_async_copy(ref, ref, sem).wait()

    lane = lax.broadcasted_iota(I32, (1, LANES), 1)
    mine = (lane // AGG_DEV) == group_low

    stage[...] = jnp.zeros_like(stage)
    pack[...] = jnp.zeros_like(pack)
    for n in range(7):
        loads[n].wait()
    w_v[...] = DAMP / d_v[...]
    s1_v[...] = w_v[...] * b_v[...]
    f1[pl.ds(0, 3), :] = s1_v[...]
    place_row = position_of(row_v[...])
    stage[pl.ds(0, 3), pl.ds(0, AGG_DEV)] = cd_v[...]
    stage[pl.ds(3, 1), pl.ds(0, AGG_DEV)] = place_row.astype(F32)
    own = stage[...]
    node_place = pick(own[3:4, :], agg_v[...])
    for n in range(BLOCKS):
        f1[pl.ds(3, 1), pl.ds(n * LANES, LANES)] = node_place[n : n + 1, :]
    own = own + pltpu.roll(own, 32, 1) + pltpu.roll(own, 64, 1) + pltpu.roll(own, 96, 1)
    e0a[group] = jnp.where(mine, own, 0.0)
    for e in range(9):
        pack[e // 4, pl.ds(32 * (e % 4), 32), pl.ds(0, NNZ)] = ca_v[e // 3, e % 3]
    pack[2, pl.ds(32, 32), pl.ds(0, NNZ)] = position_of(cq_v[...]).astype(F32)
    for n in range(3):
        rm[group, pl.ds(32 * n, 32), :] = pack[n].T[0:32, :]

    pl.semaphore_wait(barrier, CUBE - 1 + GROUPS - 1 + 2)

    def send_halo(n, own_ref, from_left, from_right):
        send(own_ref.at[:, pl.ds(NODE_DEV - WIN, WIN)], from_left, halo_send.at[n, 0], halo_recv.at[n, 0], right)
        send(own_ref.at[:, pl.ds(0, WIN)], from_right, halo_send.at[n, 1], halo_recv.at[n, 1], left)

    def wait_halo(n, from_left, from_right):
        wait_bytes(from_left, halo_recv.at[n, 0])
        wait_bytes(from_right, halo_recv.at[n, 1])

    def send_group(n, ref):
        for peer in group_peers:
            send(ref.at[group], ref.at[group], far_send.at[n], far_recv.at[n], peer)

    def send_cube(ref, send_sem, recv_sem):
        for peer in cube_peers:
            send(ref.at[member], ref.at[member], send_sem, recv_sem, peer)

    send_halo(0, f1, hl1, hr1)
    send_group(0, e0a)
    send_group(1, rm)

    loads[7].wait()
    q_s[pl.ds(24, 8), :] = jnp.zeros((8, NODE_DEV), I32)
    base = me * NODE_DEV - WIN
    for n in range(BLOCKS):
        cols = pl.ds(n * LANES, LANES)
        q_s[pl.ds(0, NNZ), cols] = q_v[:, cols] - (base + n * LANES)
    for n in range(BLOCKS):
        label = lax.broadcasted_iota(I32, (LANES, LANES), 0) % AGG_DEV
        onehot[:, pl.ds(n * LANES, LANES)] = (agg_v[pl.ds(n, 1), :] == label).astype(F32).astype(BF16)
    r_v[...] = jnp.zeros_like(r_v)
    loads[8].wait()

    def three(own_ref, from_left, from_right):
        def rows(c, n):
            if n < SIDE:
                return from_left[pl.ds(c, 1), pl.ds(n * LANES, LANES)]
            if n < SIDE + BLOCKS:
                return own_ref[pl.ds(c, 1), pl.ds((n - SIDE) * LANES, LANES)]
            return from_right[pl.ds(c, 1), pl.ds((n - SIDE - BLOCKS) * LANES, LANES)]

        return rows

    def couple_fine(rows):
        for n in range(BLOCKS):
            cols = pl.ds(n * LANES, LANES)
            sums = [None] * 3
            for k in range(4):
                near = gather_rows(q_s[pl.ds(8 * k, 8), cols], lambda r, c: rows(c, n + r), REACH)
                width = min(8, NNZ - 8 * k)
                for i in range(3):
                    term = None
                    for c in range(3):
                        part = a_v[i, c, pl.ds(8 * k, width), cols] * near[c][:width]
                        term = part if term is None else term + part
                    term = jnp.sum(term, axis=0, keepdims=True) if width < 8 else term
                    if k == 0:
                        sums[i] = term
                    elif width == 8:
                        sums[i] = sums[i] + term
                    else:
                        sums[i] = jnp.sum(sums[i], axis=0, keepdims=True) + term
            for i in range(3):
                y_v[pl.ds(i, 1), cols] = sums[i]

    wait_halo(0, hl1, hr1)
    couple_fine(three(f1, hl1, hr1))
    f2[...] = (1.0 + KEEP) * s1_v[...] + w_v[...] * y_v[...]
    send_halo(1, f2, hl2, hr2)

    for n in range(SIDE):
        idx_v[pl.ds(n, 1), :] = hl1[pl.ds(3, 1), pl.ds(n * LANES, LANES)].astype(I32)
        idx_v[pl.ds(SIDE + BLOCKS + n, 1), :] = hr1[pl.ds(3, 1), pl.ds(n * LANES, LANES)].astype(I32)
    for n in range(BLOCKS):
        idx_v[pl.ds(SIDE + n, 1), :] = f1[pl.ds(3, 1), pl.ds(n * LANES, LANES)].astype(I32)
    idx_v[pl.ds(12, 4), :] = jnp.zeros((4, LANES), I32)

    def fold(src, dst):
        for h in range(2):
            dst[member, pl.ds(4 * h, 4), :] = src[4 * h] + src[4 * h + 1] + src[4 * h + 2] + src[4 * h + 3]

    wait_bytes(e0a.at[pl.ds(0, GROUPS - 1)], far_recv.at[0])
    fold(e0a, e0b)
    send_cube(e0b, far_send.at[2], far_recv.at[2])

    wait_bytes(rm.at[pl.ds(0, GROUPS - 1)], far_recv.at[1])
    for h in range(2):
        for e4 in range(3):
            for k in range(4):
                parts = [rm[4 * h + j, pl.ds(32 * e4 + 8 * k, 8), :] for j in range(4)]
                for s in range(4):
                    e = 4 * e4 + s
                    if e > 9:
                        continue
                    whole = None
                    for j in range(4):
                        moved = parts[j] if j == s else pltpu.roll(parts[j], 32 * ((j - s) % 4), 1)
                        whole = moved if j == 0 else jnp.where((lane // 32) == j, moved, whole)
                    rows, cols = pl.ds(8 * k, 8), pl.ds(LANES * h, LANES)
                    if e < 9:
                        mx[e, rows, cols] = whole
                    else:
                        mp[rows, cols] = whole.astype(I32)

    wait_halo(1, hl2, hr2)
    couple_fine(three(f2, hl2, hr2))
    r_v[pl.ds(0, 3), :] = b_v[...] - d_v[...] * f2[...] + y_v[...]
    rest = r_v[...]
    p0 = rest.astype(BF16).astype(F32)
    rest = rest - p0
    p1 = rest.astype(BF16).astype(F32)
    pieces = jnp.concatenate([p0, p1, rest - p1], axis=0).astype(BF16)
    sums = lax.dot_general(pieces, onehot[...], (((1,), (1,)), ((), ())), preferred_element_type=F32)
    sums = sums[0:4] + sums[8:12] + sums[16:20]
    s1a[group] = jnp.where(mine, sums, 0.0)
    send_group(3, s1a)

    wait_bytes(e0b.at[pl.ds(0, CUBE - 1)], far_recv.at[2])
    inverse = None
    for r in range(CROWS):
        place = e0b[r // 2, pl.ds(4 * (r % 2) + 3, 1), :].astype(I32)
        high, low = place >> 7, place & 127
        at_high = lax.broadcasted_iota(I32, (CROWS, LANES), 0) == high
        at_low = (lax.broadcasted_iota(I32, (LANES, LANES), 0) == low).astype(F32).astype(BF16)
        weights = jnp.concatenate(
            [
                jnp.where(at_high, jnp.float32(r), 0.0),
                jnp.where(at_high, lane.astype(F32), 0.0),
            ],
            axis=0,
        ).astype(BF16)
        term = lax.dot_general(weights, at_low, (((1,), (1,)), ((), ())), preferred_element_type=F32)
        inverse = term if inverse is None else inverse + term
    inv_v[...] = (inverse[0:CROWS] * LANES + inverse[CROWS : 2 * CROWS]).astype(I32)
    for r in range(CROWS):
        for c in range(3):
            dt_v[c, pl.ds(r, 1), :] = e0b[r // 2, pl.ds(4 * (r % 2) + c, 1), :]
    for c in range(3):
        dt_v[c] = DAMP / dt_v[c]

    wait_bytes(s1a.at[pl.ds(0, GROUPS - 1)], far_recv.at[3])
    fold(s1a, s1b)
    send_cube(s1b, far_send.at[4], far_recv.at[4])
    wait_bytes(s1b.at[pl.ds(0, CUBE - 1)], far_recv.at[4])

    for t in range(CROWS // 8):
        sums = gather_rows(inv_v[pl.ds(8 * t, 8), :], lambda r, c: s1b[r // 2, pl.ds(4 * (r % 2) + c, 1), :], CROWS)
        for c in range(3):
            value = sums[c] * dt_v[c, pl.ds(8 * t, 8), :]
            for n in range(8):
                r = 8 * t + n
                cbuf[0, r // 2, pl.ds(4 * (r % 2) + c, 1), :] = value[n : n + 1, :]

    unused = lax.broadcasted_iota(I32, (8, LANES), 0) % 4 == 3
    first = jnp.where(unused, 0.0, cbuf[0, member])
    weight = jnp.where(unused, 0.0, DAMP / e0b[member])

    def sweep(n, current):
        totals = []
        for h in range(2):
            cols = pl.ds(LANES * h, LANES)
            sums = [None] * 3
            for k in range(4):
                rows = pl.ds(8 * k, 8)
                near = gather_rows(mp[rows, cols], lambda r, c: cbuf[n, r // 2, pl.ds(4 * (r % 2) + c, 1), :], CROWS)
                for i in range(3):
                    for c in range(3):
                        part = mx[3 * i + c, rows, cols] * near[c]
                        sums[i] = part if sums[i] is None else sums[i] + part
            totals += [jnp.sum(s, axis=0, keepdims=True) for s in sums]
            totals.append(jnp.zeros((1, LANES), F32))
        current = KEEP * current + first + weight * jnp.concatenate(totals, axis=0)
        cbuf[n + 1, member] = current
        send_cube(cbuf.at[n + 1], sweep_send.at[n], sweep_recv.at[n])
        wait_bytes(cbuf.at[n + 1, pl.ds(0, CUBE - 1)], sweep_recv.at[n])
        return current

    last = lax.fori_loop(0, CSWEEPS - 1, sweep, first)

    for t in range(2):
        value = gather_rows(
            idx_v[pl.ds(8 * t, 8), :], lambda r, c: cbuf[CSWEEPS - 1, r // 2, pl.ds(4 * (r % 2) + c, 1), :], CROWS
        )
        rows = three(f2, hl2, hr2)
        for n in range(8 if t == 0 else 4):
            for c in range(3):
                f3[pl.ds(c, 1), pl.ds((8 * t + n) * LANES, LANES)] = rows(c, 8 * t + n) + value[c][n : n + 1, :]
    couple_fine(lambda c, n: f3[pl.ds(c, 1), pl.ds(n * LANES, LANES)])
    f4[...] = KEEP * f3[:, pl.ds(WIN, NODE_DEV)] + s1_v[...] + w_v[...] * y_v[...]
    send_halo(2, f4, hl4, hr4)

    half = jnp.where(group_high == 0, last[0:4], last[4:8])
    moved = half
    for k in range(1, 4):
        moved = jnp.where(group_low == k, pltpu.roll(half, LANES - 32 * k, 1), moved)
    cor_o[...] = moved[0:3, 0:AGG_DEV]

    wait_halo(2, hl4, hr4)
    couple_fine(three(f4, hl4, hr4))
    sol_o[...] = KEEP * f4[...] + s1_v[...] + w_v[...] * y_v[...]

    for n, from_left in enumerate((hl1, hl2, hl4)):
        wait_bytes(from_left, halo_send.at[n, 0])
        wait_bytes(from_left, halo_send.at[n, 1])
    for n, (ref, count) in enumerate(((e0a, GROUPS), (rm, GROUPS), (e0b, CUBE), (s1a, GROUPS), (s1b, CUBE))):
        wait_bytes(ref.at[pl.ds(0, count - 1)], far_send.at[n])
    for n in range(CSWEEPS - 1):
        wait_bytes(cbuf.at[n + 1, pl.ds(0, CUBE - 1)], sweep_send.at[n])


def body(b, d, q, a, agg, row, cd, cq, ca):
    any_spec = pl.BlockSpec(memory_space=pl.ANY)
    vmem = pl.BlockSpec(memory_space=pltpu.VMEM)
    dma = pltpu.SemaphoreType.DMA
    sol, cor = pl.pallas_call(
        kernel,
        out_shape=(
            jax.ShapeDtypeStruct((3, NODE_DEV), F32),
            jax.ShapeDtypeStruct((3, AGG_DEV), F32),
        ),
        in_specs=[any_spec] * 9,
        out_specs=(vmem, vmem),
        scratch_shapes=[
            pltpu.VMEM((3, NODE_DEV), F32),
            pltpu.VMEM((3, NODE_DEV), F32),
            pltpu.VMEM((NNZ, NODE_DEV), I32),
            pltpu.VMEM((3, 3, NNZ, NODE_DEV), F32),
            pltpu.VMEM((BLOCKS, LANES), I32),
            pltpu.VMEM((1, AGG_DEV), I32),
            pltpu.VMEM((3, AGG_DEV), F32),
            pltpu.VMEM((AGG_DEV, NNZ), I32),
            pltpu.VMEM((3, 3, AGG_DEV, NNZ), F32),
            pltpu.VMEM((3, NODE_DEV), F32),
            pltpu.VMEM((3, NODE_DEV), F32),
            pltpu.VMEM((32, NODE_DEV), I32),
            pltpu.VMEM((3, NODE_DEV), F32),
            pltpu.VMEM((8, NODE_DEV), F32),
            pltpu.VMEM((LANES, NODE_DEV), BF16),
            pltpu.VMEM((16, LANES), I32),
            pltpu.VMEM((4, NODE_DEV), F32),
            pltpu.VMEM((4, WIN), F32),
            pltpu.VMEM((4, WIN), F32),
            pltpu.VMEM((3, NODE_DEV), F32),
            pltpu.VMEM((3, WIN), F32),
            pltpu.VMEM((3, WIN), F32),
            pltpu.VMEM((3, NODE_DEV + 2 * WIN), F32),
            pltpu.VMEM((3, NODE_DEV), F32),
            pltpu.VMEM((3, WIN), F32),
            pltpu.VMEM((3, WIN), F32),
            pltpu.VMEM((4, LANES), F32),
            pltpu.VMEM((GROUPS, 4, LANES), F32),
            pltpu.VMEM((CUBE, 8, LANES), F32),
            pltpu.VMEM((GROUPS, 4, LANES), F32),
            pltpu.VMEM((CUBE, 8, LANES), F32),
            pltpu.VMEM((3, LANES, LANES), F32),
            pltpu.VMEM((GROUPS, 96, LANES), F32),
            pltpu.VMEM((9, 32, 2 * LANES), F32),
            pltpu.VMEM((32, 2 * LANES), I32),
            pltpu.VMEM((CROWS, LANES), I32),
            pltpu.VMEM((3, CROWS, LANES), F32),
            pltpu.VMEM((CSWEEPS, CUBE, 8, LANES), F32),
            dma((9,)),
            dma((3, 2)),
            dma((3, 2)),
            dma((5,)),
            dma((5,)),
            dma((CSWEEPS - 1,)),
            dma((CSWEEPS - 1,)),
        ],
        compiler_params=pltpu.CompilerParams(collective_id=0, has_side_effects=True),
        name="vcycle",
    )(
        b.T,
        d.T,
        q.T,
        a.transpose(2, 3, 1, 0),
        agg.reshape(BLOCKS, LANES),
        row.reshape(1, AGG_DEV),
        cd.T,
        cq,
        ca.transpose(2, 3, 0, 1),
    )
    return sol.T, cor.T


def solution(mesh):
    rows, line = P("dom", None), P("dom")
    blocks = P("dom", None, None, None)
    return jax.shard_map(
        body,
        mesh=mesh,
        in_specs=(rows, rows, rows, blocks, line, line, rows, rows, blocks),
        out_specs=(rows, rows),
        check_vma=False,
    )
```

time: 764 us -> 64.9 us (0.08)
  the two profiles are of different devices: /device:TPU:1 before, /device:TPU:0 now
where the time goes in v1:
time: 64.9 us; the launch traced here: 64.6 us
  Pallas kernels  61.4 us (95%)
  local copies, waits for them, and re-layouts  2.56 us (4%)
    pallas_call x1, Pallas kernels, body(): pl.pallas_call(kernel, out_shape=(jax.ShapeDtypeStruct((3, NODE_DEV), F32...  61.4 us
    unnamed x2, local copies, waits for them, and re-layouts  2.56 us

profile of v1, /device:TPU:0, one launch (start us, length us, event | category | flops | bytes accessed | tf_op | source)
XLA Modules:
  0.0 64.6 jit_solution(9110076167280669262)
XLA Ops:
  0.6 61.4 %vcycle.1 = (f32[3,1024]{1,0:T(4,128)}, f32[3,32]{1,0:T(4,128)}) custom-call(f32[3,1024]{1,0:T(4,128)} %bitcast.13, f32[3,1024]{1,0:T(4,128)} %bitcast.14, s32[27,1024]{1,0:T(8,128)} %bitcast.12, f32[3,3,27,1024]{3,2,1,0:T(8,128)} %bitcast.10, s32[8,128]{1,0:T(8,128)} %bitcast.16, s32[1,32]{1,0:T(1,128)} %bitcast.19, f32[3,32]{1,0:T(4,128)} %bitcast.17, ...), custom_call_target="tpu_custom_call" | custom-call | tf_op jit(solution)/shard_map/vcycle/pallas_call | solution.py:352
  62.0 1.3 %copy.13 = f32[1024,3]{0,1:T(4,128)} copy(f32[1024,3]{0,1:T(4,128)} %bitcast.15) | data formatting | bytes 24576
  63.4 1.2 %copy.14 = f32[32,3]{0,1:T(4,128)} copy(f32[32,3]{0,1:T(4,128)} %bitcast.18) | data formatting | bytes 768

commit v2 on v1

--- a/solution.py
+++ b/solution.py
@@ -60,9 +60,9 @@
     b_v, d_v, q_v, a_v, agg_v, row_v, cd_v, cq_v, ca_v,
     w_v, s1_v, q_s, y_v, r_v, onehot, idx_v,
     f1, hl1, hr1, f2, hl2, hr2, f3, f4, hl4, hr4,
-    stage, e0a, e0b, s1a, s1b,
+    stage, far0, far1, tab0, tab1,
     pack, rm, mx, mp,
-    inv_v, dt_v, cbuf,
+    inv_v, wbuf, cbuf,
     load_sem, halo_send, halo_recv, far_send, far_recv, sweep_send, sweep_recv,
 ):
     me = lax.axis_index("dom")
@@ -81,6 +81,19 @@
                 other = other + (1 - 2 * bit(p)) * (1 << p)
         return other
 
+    def ring(low, high):
+        at = bit(high) * 2 + bit(low)
+        places = [(at + k) % 4 for k in range(4)]
+        return [(v // 2) * (1 << high) + (v % 2) * (1 << low) for v in places]
+
+    along_x, along_z, along_y = ring(1, 2), ring(3, 4), ring(5, 6)
+    cores = [bit(0), 1 - bit(0)]
+    steps = [(x, z, y, c) for x in range(4) for z in range(4) for y in range(4) for c in range(2)]
+    hops = (0, 1, 2, 1)
+    steps = sorted(steps, key=lambda v: -(hops[v[0]] + hops[v[1]] + hops[v[2]]) - 0.5 * v[3])
+    all_peers = [along_x[x] + along_z[z] + along_y[y] + cores[c] for x, z, y, c in steps if (x, z, y, c) != (0, 0, 0, 0)]
+    my_high = member * 2 + bit(6)
+    my_slot = ((my_high // 8) * 4 + group_low) * 8 + my_high % 8
     cube_peers = [flipped(CUBE_BITS, k) for k in range(1, CUBE)]
     group_peers = [flipped(GROUP_BITS, k) for k in range(1, GROUPS)]
     left, right = (me + DEVICES - 1) % DEVICES, (me + 1) % DEVICES
@@ -97,7 +110,7 @@
         loads.append(copy)
 
     barrier = pltpu.get_barrier_semaphore()
-    for peer in cube_peers + group_peers + [left, right]:
+    for peer in all_peers:
         pl.semaphore_signal(barrier, inc=1, device_id=(peer,), device_id_type=MESH)
 
     def send(src, dst, send_sem, recv_sem, peer):
@@ -110,7 +123,6 @@
         pltpu.make_async_copy(ref, ref, sem).wait()
 
     lane = lax.broadcasted_iota(I32, (1, LANES), 1)
-    mine = (lane // AGG_DEV) == group_low
 
     stage[...] = jnp.zeros_like(stage)
     pack[...] = jnp.zeros_like(pack)
@@ -126,15 +138,17 @@
     node_place = pick(own[3:4, :], agg_v[...])
     for n in range(BLOCKS):
         f1[pl.ds(3, 1), pl.ds(n * LANES, LANES)] = node_place[n : n + 1, :]
-    own = own + pltpu.roll(own, 32, 1) + pltpu.roll(own, 64, 1) + pltpu.roll(own, 96, 1)
-    e0a[group] = jnp.where(mine, own, 0.0)
+    line = own[0:1]
+    for n in range(1, 4):
+        line = jnp.where(lane // AGG_DEV == n, pltpu.roll(own, 32 * n, 1)[n : n + 1], line)
+    far0[my_slot] = line
     for e in range(9):
         pack[e // 4, pl.ds(32 * (e % 4), 32), pl.ds(0, NNZ)] = ca_v[e // 3, e % 3]
     pack[2, pl.ds(32, 32), pl.ds(0, NNZ)] = position_of(cq_v[...]).astype(F32)
     for n in range(3):
         rm[group, pl.ds(32 * n, 32), :] = pack[n].T[0:32, :]
 
-    pl.semaphore_wait(barrier, CUBE - 1 + GROUPS - 1 + 2)
+    pl.semaphore_wait(barrier, DEVICES - 1)
 
     def send_halo(n, own_ref, from_left, from_right):
         send(own_ref.at[:, pl.ds(NODE_DEV - WIN, WIN)], from_left, halo_send.at[n, 0], halo_recv.at[n, 0], right)
@@ -148,12 +162,27 @@
         for peer in group_peers:
             send(ref.at[group], ref.at[group], far_send.at[n], far_recv.at[n], peer)
 
+    def send_all(n, ref):
+        for peer in all_peers:
+            send(ref.at[my_slot], ref.at[my_slot], far_send.at[n], far_recv.at[n], peer)
+
+    def receive_all(n, ref, table):
+        wait_bytes(ref.at[pl.ds(0, DEVICES - 1)], far_recv.at[n])
+        for t in range(4):
+            parts = [ref[pl.ds(32 * t + 8 * j, 8), 0, :] for j in range(4)]
+            for c in range(table.shape[0]):
+                whole = None
+                for j in range(4):
+                    moved = parts[j] if j == c else pltpu.roll(parts[j], 32 * ((j - c) % 4), 1)
+                    whole = moved if j == 0 else jnp.where((lane // 32) == j, moved, whole)
+                table[c, pl.ds(8 * t, 8), :] = whole
+
     def send_cube(ref, send_sem, recv_sem):
         for peer in cube_peers:
             send(ref.at[member], ref.at[member], send_sem, recv_sem, peer)
 
     send_halo(0, f1, hl1, hr1)
-    send_group(0, e0a)
+    send_all(0, far0)
     send_group(1, rm)
 
     loads[7].wait()
@@ -212,14 +241,44 @@
         idx_v[pl.ds(SIDE + n, 1), :] = f1[pl.ds(3, 1), pl.ds(n * LANES, LANES)].astype(I32)
     idx_v[pl.ds(12, 4), :] = jnp.zeros((4, LANES), I32)
 
-    def fold(src, dst):
-        for h in range(2):
-            dst[member, pl.ds(4 * h, 4), :] = src[4 * h] + src[4 * h + 1] + src[4 * h + 2] + src[4 * h + 3]
-
-    wait_bytes(e0a.at[pl.ds(0, GROUPS - 1)], far_recv.at[0])
-    fold(e0a, e0b)
-    send_cube(e0b, far_send.at[2], far_recv.at[2])
-
+    wait_halo(1, hl2, hr2)
+    couple_fine(three(f2, hl2, hr2))
+    r_v[pl.ds(0, 3), :] = b_v[...] - d_v[...] * f2[...] + y_v[...]
+    rest = r_v[...]
+    p0 = rest.astype(BF16).astype(F32)
+    rest = rest - p0
+    p1 = rest.astype(BF16).astype(F32)
+    pieces = jnp.concatenate([p0, p1, rest - p1], axis=0).astype(BF16)
+    sums = lax.dot_general(pieces, onehot[...], (((1,), (1,)), ((), ())), preferred_element_type=F32)
+    sums = sums[0:4] + sums[8:12] + sums[16:20]
+    line = sums[0:1]
+    for n in range(1, 3):
+        line = jnp.where(lane // AGG_DEV == n, sums[n : n + 1], line)
+    far1[my_slot] = line
+    send_all(2, far1)
+
+    receive_all(0, far0, tab0)
+    inverse = None
+    for r in range(CROWS):
+        place = tab0[3, pl.ds(r, 1), :].astype(I32)
+        high, low = place >> 7, place & 127
+        at_high = lax.broadcasted_iota(I32, (CROWS, LANES), 0) == high
+        at_low = (lax.broadcasted_iota(I32, (LANES, LANES), 0) == low).astype(F32).astype(BF16)
+        weights = jnp.concatenate(
+            [
+                jnp.where(at_high, jnp.float32(r), 0.0),
+                jnp.where(at_high, lane.astype(F32), 0.0),
+            ],
+            axis=0,
+        ).astype(BF16)
+        term = lax.dot_general(weights, at_low, (((1,), (1,)), ((), ())), preferred_element_type=F32)
+        inverse = term if inverse is None else inverse + term
+    inv_v[...] = (inverse[0:CROWS] * LANES + inverse[CROWS : 2 * CROWS]).astype(I32)
+    for c in range(3):
+        tab0[c] = DAMP / tab0[c]
+    for r in range(CROWS):
+        for c in range(3):
+            wbuf[r // 2, pl.ds(4 * (r % 2) + c, 1), :] = tab0[c, pl.ds(r, 1), :]
     wait_bytes(rm.at[pl.ds(0, GROUPS - 1)], far_recv.at[1])
     for h in range(2):
         for e4 in range(3):
@@ -239,58 +298,19 @@
                     else:
                         mp[rows, cols] = whole.astype(I32)
 
-    wait_halo(1, hl2, hr2)
-    couple_fine(three(f2, hl2, hr2))
-    r_v[pl.ds(0, 3), :] = b_v[...] - d_v[...] * f2[...] + y_v[...]
-    rest = r_v[...]
-    p0 = rest.astype(BF16).astype(F32)
-    rest = rest - p0
-    p1 = rest.astype(BF16).astype(F32)
-    pieces = jnp.concatenate([p0, p1, rest - p1], axis=0).astype(BF16)
-    sums = lax.dot_general(pieces, onehot[...], (((1,), (1,)), ((), ())), preferred_element_type=F32)
-    sums = sums[0:4] + sums[8:12] + sums[16:20]
-    s1a[group] = jnp.where(mine, sums, 0.0)
-    send_group(3, s1a)
-
-    wait_bytes(e0b.at[pl.ds(0, CUBE - 1)], far_recv.at[2])
-    inverse = None
-    for r in range(CROWS):
-        place = e0b[r // 2, pl.ds(4 * (r % 2) + 3, 1), :].astype(I32)
-        high, low = place >> 7, place & 127
-        at_high = lax.broadcasted_iota(I32, (CROWS, LANES), 0) == high
-        at_low = (lax.broadcasted_iota(I32, (LANES, LANES), 0) == low).astype(F32).astype(BF16)
-        weights = jnp.concatenate(
-            [
-                jnp.where(at_high, jnp.float32(r), 0.0),
-                jnp.where(at_high, lane.astype(F32), 0.0),
-            ],
-            axis=0,
-        ).astype(BF16)
-        term = lax.dot_general(weights, at_low, (((1,), (1,)), ((), ())), preferred_element_type=F32)
-        inverse = term if inverse is None else inverse + term
-    inv_v[...] = (inverse[0:CROWS] * LANES + inverse[CROWS : 2 * CROWS]).astype(I32)
-    for r in range(CROWS):
+    receive_all(2, far1, tab1)
+
+    for t in range(CROWS // 8):
+        sums = gather_rows(inv_v[pl.ds(8 * t, 8), :], lambda r, c: tab1[c, pl.ds(r, 1), :], CROWS)
         for c in range(3):
-            dt_v[c, pl.ds(r, 1), :] = e0b[r // 2, pl.ds(4 * (r % 2) + c, 1), :]
-    for c in range(3):
-        dt_v[c] = DAMP / dt_v[c]
-
-    wait_bytes(s1a.at[pl.ds(0, GROUPS - 1)], far_recv.at[3])
-    fold(s1a, s1b)
-    send_cube(s1b, far_send.at[4], far_recv.at[4])
-    wait_bytes(s1b.at[pl.ds(0, CUBE - 1)], far_recv.at[4])
-
-    for t in range(CROWS // 8):
-        sums = gather_rows(inv_v[pl.ds(8 * t, 8), :], lambda r, c: s1b[r // 2, pl.ds(4 * (r % 2) + c, 1), :], CROWS)
-        for c in range(3):
-            value = sums[c] * dt_v[c, pl.ds(8 * t, 8), :]
+            value = sums[c] * tab0[c, pl.ds(8 * t, 8), :]
             for n in range(8):
                 r = 8 * t + n
                 cbuf[0, r // 2, pl.ds(4 * (r % 2) + c, 1), :] = value[n : n + 1, :]
 
     unused = lax.broadcasted_iota(I32, (8, LANES), 0) % 4 == 3
     first = jnp.where(unused, 0.0, cbuf[0, member])
-    weight = jnp.where(unused, 0.0, DAMP / e0b[member])
+    weight = jnp.where(unused, 0.0, wbuf[member])
 
     def sweep(n, current):
         totals = []
@@ -339,7 +359,7 @@
     for n, from_left in enumerate((hl1, hl2, hl4)):
         wait_bytes(from_left, halo_send.at[n, 0])
         wait_bytes(from_left, halo_send.at[n, 1])
-    for n, (ref, count) in enumerate(((e0a, GROUPS), (rm, GROUPS), (e0b, CUBE), (s1a, GROUPS), (s1b, CUBE))):
+    for n, (ref, count) in enumerate(((far0, DEVICES), (rm, GROUPS), (far1, DEVICES))):
         wait_bytes(ref.at[pl.ds(0, count - 1)], far_send.at[n])
     for n in range(CSWEEPS - 1):
         wait_bytes(cbuf.at[n + 1, pl.ds(0, CUBE - 1)], sweep_send.at[n])
@@ -385,22 +405,22 @@
             pltpu.VMEM((3, WIN), F32),
             pltpu.VMEM((3, WIN), F32),
             pltpu.VMEM((4, LANES), F32),
-            pltpu.VMEM((GROUPS, 4, LANES), F32),
-            pltpu.VMEM((CUBE, 8, LANES), F32),
-            pltpu.VMEM((GROUPS, 4, LANES), F32),
-            pltpu.VMEM((CUBE, 8, LANES), F32),
+            pltpu.VMEM((DEVICES, 1, LANES), F32),
+            pltpu.VMEM((DEVICES, 1, LANES), F32),
+            pltpu.VMEM((4, CROWS, LANES), F32),
+            pltpu.VMEM((3, CROWS, LANES), F32),
             pltpu.VMEM((3, LANES, LANES), F32),
             pltpu.VMEM((GROUPS, 96, LANES), F32),
             pltpu.VMEM((9, 32, 2 * LANES), F32),
             pltpu.VMEM((32, 2 * LANES), I32),
             pltpu.VMEM((CROWS, LANES), I32),
-            pltpu.VMEM((3, CROWS, LANES), F32),
+            pltpu.VMEM((CUBE, 8, LANES), F32),
             pltpu.VMEM((CSWEEPS, CUBE, 8, LANES), F32),
             dma((9,)),
             dma((3, 2)),
             dma((3, 2)),
-            dma((5,)),
-            dma((5,)),
+            dma((3,)),
+            dma((3,)),
             dma((CSWEEPS - 1,)),
             dma((CSWEEPS - 1,)),
         ],

time: 64.9 us -> 61.6 us (0.949)
  Pallas kernels: 61.4 us -> 58.2 us
    pallas_call x1, Pallas kernels: 61.4 us -> 58.2 us  [body(): pl.pallas_call(kernel, out_shape=(jax.ShapeDtypeStruct((3, NODE_DEV), F32...]
where the time goes in v2:
time: 61.6 us; the launch traced here: 61.4 us
  Pallas kernels  58.2 us (94%)
  local copies, waits for them, and re-layouts  2.56 us (4%)
  between operations  0.64 us (1%)
    pallas_call x1, Pallas kernels, body(): pl.pallas_call(kernel, out_shape=(jax.ShapeDtypeStruct((3, NODE_DEV), F32...  58.2 us
    unnamed x2, local copies, waits for them, and re-layouts  2.56 us

profile of v2, /device:TPU:0, one launch (start us, length us, event | category | flops | bytes accessed | tf_op | source)
XLA Modules:
  0.0 61.4 jit_solution(15588526233986083766)
XLA Ops:
  0.6 58.2 %vcycle.1 = (f32[3,1024]{1,0:T(4,128)}, f32[3,32]{1,0:T(4,128)}) custom-call(f32[3,1024]{1,0:T(4,128)} %bitcast.13, f32[3,1024]{1,0:T(4,128)} %bitcast.14, s32[27,1024]{1,0:T(8,128)} %bitcast.12, f32[3,3,27,1024]{3,2,1,0:T(8,128)} %bitcast.10, s32[8,128]{1,0:T(8,128)} %bitcast.16, s32[1,32]{1,0:T(1,128)} %bitcast.19, f32[3,32]{1,0:T(4,128)} %bitcast.17, ...), custom_call_target="tpu_custom_call" | custom-call | tf_op jit(solution)/shard_map/vcycle/pallas_call | solution.py:372
  58.9 1.3 %copy.13 = f32[1024,3]{0,1:T(4,128)} copy(f32[1024,3]{0,1:T(4,128)} %bitcast.15) | data formatting | bytes 24576
  60.2 1.2 %copy.14 = f32[32,3]{0,1:T(4,128)} copy(f32[32,3]{0,1:T(4,128)} %bitcast.18) | data formatting | bytes 768

commit v3 on v2

--- a/solution.py
+++ b/solution.py
@@ -14,14 +14,15 @@
 LANES = 128
 BLOCKS = NODE_DEV // LANES
 SIDE = WIN // LANES
+WIDE = BLOCKS + 2 * SIDE
 REACH = 2 * SIDE + 1
 CUBE = 16
 GROUPS = 8
 CROWS = 32
 DAMP = 0.7
 KEEP = 1.0 - DAMP
-CUBE_BITS = (0, 1, 3, 5)
-GROUP_BITS = (2, 4, 6)
+CUBE_BITS = ((0,), (1,), (3,), (5,))
+GROUP_BITS = ((1, 2), (3, 4), (5, 6))
 MESH = pl.DeviceIdType.MESH
 F32, I32, BF16 = jnp.float32, jnp.int32, jnp.bfloat16
 
@@ -30,7 +31,7 @@
     def bit(p):
         return (row >> p) & 1
 
-    high = bit(10) * 16 + bit(8) * 8 + bit(6) * 4 + bit(5) * 2 + bit(11)
+    high = (bit(10) ^ bit(11)) * 16 + (bit(8) ^ bit(9)) * 8 + (bit(6) ^ bit(7)) * 4 + bit(5) * 2 + bit(11)
     lane = bit(9) * 64 + bit(7) * 32 + (row & 31)
     return high * LANES + lane
 
@@ -58,19 +59,19 @@
     b_h, d_h, q_h, a_h, agg_h, row_h, cd_h, cq_h, ca_h,
     sol_o, cor_o,
     b_v, d_v, q_v, a_v, agg_v, row_v, cd_v, cq_v, ca_v,
-    w_v, s1_v, q_s, y_v, r_v, onehot, idx_v,
-    f1, hl1, hr1, f2, hl2, hr2, f3, f4, hl4, hr4,
+ q_s, y_v, r_v, onehot, idx_v,
+    f1, f1l, f1r, f2, f3, f4,
     stage, far0, far1, tab0, tab1,
     pack, rm, mx, mp,
     inv_v, wbuf, cbuf,
-    load_sem, halo_send, halo_recv, far_send, far_recv, sweep_send, sweep_recv,
+    load_sem, side_send, side_recv, entered, far_send, far_recv, sweep_send, sweep_recv,
 ):
     me = lax.axis_index("dom")
 
     def bit(p):
         return (me // (1 << p)) % 2
 
-    member = bit(5) * 8 + bit(3) * 4 + bit(1) * 2 + bit(0)
+    member = (bit(5) + bit(6)) % 2 * 8 + (bit(3) + bit(4)) % 2 * 4 + (bit(1) + bit(2)) % 2 * 2 + bit(0)
     group = bit(6) * 4 + bit(4) * 2 + bit(2)
     group_low, group_high = bit(4) * 2 + bit(2), bit(6)
 
@@ -78,7 +79,8 @@
         other = me
         for n, p in enumerate(bits):
             if (k >> n) & 1:
-                other = other + (1 - 2 * bit(p)) * (1 << p)
+                for q in p:
+                    other = other + (1 - 2 * bit(q)) * (1 << q)
         return other
 
     def ring(low, high):
@@ -110,7 +112,7 @@
         loads.append(copy)
 
     barrier = pltpu.get_barrier_semaphore()
-    for peer in all_peers:
+    for peer in cube_peers + group_peers + [left, right]:
         pl.semaphore_signal(barrier, inc=1, device_id=(peer,), device_id_type=MESH)
 
     def send(src, dst, send_sem, recv_sem, peer):
@@ -124,39 +126,68 @@
 
     lane = lax.broadcasted_iota(I32, (1, LANES), 1)
 
+    def cols(n, count=1):
+        return pl.ds(n * LANES, count * LANES)
+
+    for n in range(4):
+        loads[n].wait()
+    place_row = position_of(row_v[...])
     stage[...] = jnp.zeros_like(stage)
-    pack[...] = jnp.zeros_like(pack)
-    for n in range(7):
+    stage[pl.ds(3, 1), pl.ds(0, AGG_DEV)] = place_row.astype(F32)
+    node_place = pick(stage[pl.ds(3, 1), :], agg_v[...])
+    w0 = DAMP / d_v[...]
+    f1[pl.ds(0, 3), :] = w0 * b_v[...]
+    f1[pl.ds(4, 3), :] = w0
+    for n in range(BLOCKS):
+        f1[pl.ds(3, 1), cols(n)] = node_place[n : n + 1, :]
+    for n in range(4, 9):
         loads[n].wait()
-    w_v[...] = DAMP / d_v[...]
-    s1_v[...] = w_v[...] * b_v[...]
-    f1[pl.ds(0, 3), :] = s1_v[...]
-    place_row = position_of(row_v[...])
+    pl.semaphore_wait(barrier, CUBE - 1 + GROUPS - 1 + 2)
+
+    def to_right(n, src, dst):
+        return pltpu.make_async_remote_copy(
+            src_ref=src, dst_ref=dst, send_sem=side_send.at[n, 0], recv_sem=side_recv.at[n, 0],
+            device_id=(right,), device_id_type=MESH,
+        )
+
+    def to_left(n, src, dst):
+        return pltpu.make_async_remote_copy(
+            src_ref=src, dst_ref=dst, send_sem=side_send.at[n, 1], recv_sem=side_recv.at[n, 1],
+            device_id=(left,), device_id_type=MESH,
+        )
+
+    own_end, own_start = pl.ds(NODE_DEV, WIN), pl.ds(WIN, WIN)
+    from_left, from_right = pl.ds(0, WIN), pl.ds(NODE_DEV + WIN, WIN)
+    rightward = [
+        to_right(0, f1.at[:, pl.ds(NODE_DEV - WIN, WIN)], f1l),
+        to_right(1, f2.at[:, own_end], f2.at[:, from_left]),
+        to_right(2, f4.at[:, own_end], f4.at[:, from_left]),
+    ]
+    leftward = [
+        to_left(0, f1.at[:, pl.ds(0, WIN)], f1r),
+        to_left(1, f2.at[:, own_start], f2.at[:, from_right]),
+        to_left(2, f4.at[:, own_start], f4.at[:, from_right]),
+    ]
+    has_left, has_right = me > 0, me < DEVICES - 1
+
+    def start_sides(n):
+        pl.when(has_right)(rightward[n].start)
+        pl.when(has_left)(leftward[n].start)
+
+    def await_sides(n):
+        pl.when(has_left)(rightward[n].wait_recv)
+        pl.when(has_right)(leftward[n].wait_recv)
+
+    start_sides(0)
+    for peer in group_peers:
+        pl.semaphore_signal(entered, inc=1, device_id=(peer,), device_id_type=MESH)
+
     stage[pl.ds(0, 3), pl.ds(0, AGG_DEV)] = cd_v[...]
-    stage[pl.ds(3, 1), pl.ds(0, AGG_DEV)] = place_row.astype(F32)
     own = stage[...]
-    node_place = pick(own[3:4, :], agg_v[...])
-    for n in range(BLOCKS):
-        f1[pl.ds(3, 1), pl.ds(n * LANES, LANES)] = node_place[n : n + 1, :]
     line = own[0:1]
     for n in range(1, 4):
         line = jnp.where(lane // AGG_DEV == n, pltpu.roll(own, 32 * n, 1)[n : n + 1], line)
     far0[my_slot] = line
-    for e in range(9):
-        pack[e // 4, pl.ds(32 * (e % 4), 32), pl.ds(0, NNZ)] = ca_v[e // 3, e % 3]
-    pack[2, pl.ds(32, 32), pl.ds(0, NNZ)] = position_of(cq_v[...]).astype(F32)
-    for n in range(3):
-        rm[group, pl.ds(32 * n, 32), :] = pack[n].T[0:32, :]
-
-    pl.semaphore_wait(barrier, DEVICES - 1)
-
-    def send_halo(n, own_ref, from_left, from_right):
-        send(own_ref.at[:, pl.ds(NODE_DEV - WIN, WIN)], from_left, halo_send.at[n, 0], halo_recv.at[n, 0], right)
-        send(own_ref.at[:, pl.ds(0, WIN)], from_right, halo_send.at[n, 1], halo_recv.at[n, 1], left)
-
-    def wait_halo(n, from_left, from_right):
-        wait_bytes(from_left, halo_recv.at[n, 0])
-        wait_bytes(from_right, halo_recv.at[n, 1])
 
     def send_group(n, ref):
         for peer in group_peers:
@@ -181,43 +212,36 @@
         for peer in cube_peers:
             send(ref.at[member], ref.at[member], send_sem, recv_sem, peer)
 
-    send_halo(0, f1, hl1, hr1)
-    send_all(0, far0)
+    def number_columns(n, carry):
+        here = pl.ds(pl.multiple_of(n * LANES, LANES), LANES)
+        q_s[pl.ds(24, 8), here] = jnp.zeros((8, LANES), I32)
+        q_s[pl.ds(0, NNZ), here] = q_v[:, here] - (me * NODE_DEV - WIN + n * LANES)
+        return carry
+
+    def pack_one(e, carry):
+        pack[e // 4, pl.ds(pl.multiple_of(32 * (e % 4), 32), 32), pl.ds(0, NNZ)] = ca_v[e // 3, e % 3]
+        return carry
+
+    pack[...] = jnp.zeros_like(pack)
+    lax.fori_loop(0, 9, pack_one, 0)
+    pack[2, pl.ds(32, 32), pl.ds(0, NNZ)] = position_of(cq_v[...]).astype(F32)
+    for n in range(3):
+        rm[group, pl.ds(32 * n, 32), :] = pack[n].T[0:32, :]
     send_group(1, rm)
 
-    loads[7].wait()
-    q_s[pl.ds(24, 8), :] = jnp.zeros((8, NODE_DEV), I32)
-    base = me * NODE_DEV - WIN
-    for n in range(BLOCKS):
-        cols = pl.ds(n * LANES, LANES)
-        q_s[pl.ds(0, NNZ), cols] = q_v[:, cols] - (base + n * LANES)
-    for n in range(BLOCKS):
-        label = lax.broadcasted_iota(I32, (LANES, LANES), 0) % AGG_DEV
-        onehot[:, pl.ds(n * LANES, LANES)] = (agg_v[pl.ds(n, 1), :] == label).astype(F32).astype(BF16)
-    r_v[...] = jnp.zeros_like(r_v)
-    loads[8].wait()
-
-    def three(own_ref, from_left, from_right):
-        def rows(c, n):
-            if n < SIDE:
-                return from_left[pl.ds(c, 1), pl.ds(n * LANES, LANES)]
-            if n < SIDE + BLOCKS:
-                return own_ref[pl.ds(c, 1), pl.ds((n - SIDE) * LANES, LANES)]
-            return from_right[pl.ds(c, 1), pl.ds((n - SIDE - BLOCKS) * LANES, LANES)]
-
-        return rows
-
-    def couple_fine(rows):
-        for n in range(BLOCKS):
-            cols = pl.ds(n * LANES, LANES)
+    lax.fori_loop(0, BLOCKS, number_columns, 0)
+
+    def couple_fine(blocks, field):
+        for n in blocks:
+            here = cols(n - SIDE)
             sums = [None] * 3
             for k in range(4):
-                near = gather_rows(q_s[pl.ds(8 * k, 8), cols], lambda r, c: rows(c, n + r), REACH)
+                near = gather_rows(q_s[pl.ds(8 * k, 8), here], lambda r, c: field(c, n + r - SIDE), REACH)
                 width = min(8, NNZ - 8 * k)
                 for i in range(3):
                     term = None
                     for c in range(3):
-                        part = a_v[i, c, pl.ds(8 * k, width), cols] * near[c][:width]
+                        part = a_v[i, c, pl.ds(8 * k, width), here] * near[c][:width]
                         term = part if term is None else term + part
                     term = jnp.sum(term, axis=0, keepdims=True) if width < 8 else term
                     if k == 0:
@@ -227,23 +251,44 @@
                     else:
                         sums[i] = jnp.sum(sums[i], axis=0, keepdims=True) + term
             for i in range(3):
-                y_v[pl.ds(i, 1), cols] = sums[i]
-
-    wait_halo(0, hl1, hr1)
-    couple_fine(three(f1, hl1, hr1))
-    f2[...] = (1.0 + KEEP) * s1_v[...] + w_v[...] * y_v[...]
-    send_halo(1, f2, hl2, hr2)
-
-    for n in range(SIDE):
-        idx_v[pl.ds(n, 1), :] = hl1[pl.ds(3, 1), pl.ds(n * LANES, LANES)].astype(I32)
-        idx_v[pl.ds(SIDE + BLOCKS + n, 1), :] = hr1[pl.ds(3, 1), pl.ds(n * LANES, LANES)].astype(I32)
-    for n in range(BLOCKS):
-        idx_v[pl.ds(SIDE + n, 1), :] = f1[pl.ds(3, 1), pl.ds(n * LANES, LANES)].astype(I32)
-    idx_v[pl.ds(12, 4), :] = jnp.zeros((4, LANES), I32)
-
-    wait_halo(1, hl2, hr2)
-    couple_fine(three(f2, hl2, hr2))
-    r_v[pl.ds(0, 3), :] = b_v[...] - d_v[...] * f2[...] + y_v[...]
+                y_v[pl.ds(i, 1), here] = sums[i]
+
+    def first_field(row, n, count=1):
+        if n < SIDE:
+            return f1l[row, cols(n, count)]
+        if n < SIDE + BLOCKS:
+            return f1[row, cols(n - SIDE, count)]
+        return f1r[row, cols(n - SIDE - BLOCKS, count)]
+
+    def start_field(c, n):
+        return first_field(pl.ds(c, 1), n)
+
+    middle = range(2 * SIDE, BLOCKS)
+    border = [*range(SIDE, 2 * SIDE), *range(BLOCKS, BLOCKS + SIDE)]
+    values, weights_at = pl.ds(0, 3), pl.ds(4, 3)
+
+    couple_fine(middle, start_field)
+    pl.semaphore_wait(entered, GROUPS - 1)
+    send_all(0, far0)
+
+    await_sides(0)
+    couple_fine(border, start_field)
+    inside = cols(SIDE, BLOCKS)
+    f2[:, inside] = (1.0 + KEEP) * f1[values, :] + f1[weights_at, :] * y_v[...]
+    start_sides(1)
+    couple_fine(middle, lambda c, n: f2[pl.ds(c, 1), cols(n)])
+
+    def label_block(n, carry):
+        label = lax.broadcasted_iota(I32, (LANES, LANES), 0) % AGG_DEV
+        hit = agg_v[pl.ds(n, 1), :] == label
+        onehot[:, pl.ds(pl.multiple_of(n * LANES, LANES), LANES)] = hit.astype(F32).astype(BF16)
+        return carry
+
+    lax.fori_loop(0, BLOCKS, label_block, 0)
+    r_v[...] = jnp.zeros_like(r_v)
+    await_sides(1)
+    couple_fine(border, lambda c, n: f2[pl.ds(c, 1), cols(n)])
+    r_v[pl.ds(0, 3), :] = b_v[...] - d_v[...] * f2[:, inside] + y_v[...]
     rest = r_v[...]
     p0 = rest.astype(BF16).astype(F32)
     rest = rest - p0
@@ -292,11 +337,15 @@
                     for j in range(4):
                         moved = parts[j] if j == s else pltpu.roll(parts[j], 32 * ((j - s) % 4), 1)
                         whole = moved if j == 0 else jnp.where((lane // 32) == j, moved, whole)
-                    rows, cols = pl.ds(8 * k, 8), pl.ds(LANES * h, LANES)
+                    rows, lines = pl.ds(8 * k, 8), pl.ds(LANES * h, LANES)
                     if e < 9:
-                        mx[e, rows, cols] = whole
+                        mx[e, rows, lines] = whole
                     else:
-                        mp[rows, cols] = whole.astype(I32)
+                        mp[rows, lines] = whole.astype(I32)
+
+    idx_v[...] = jnp.zeros_like(idx_v)
+    for n in range(WIDE):
+        idx_v[pl.ds(n, 1), :] = first_field(pl.ds(3, 1), n).astype(I32)
 
     receive_all(2, far1, tab1)
 
@@ -315,14 +364,14 @@
     def sweep(n, current):
         totals = []
         for h in range(2):
-            cols = pl.ds(LANES * h, LANES)
+            lines = pl.ds(LANES * h, LANES)
             sums = [None] * 3
             for k in range(4):
                 rows = pl.ds(8 * k, 8)
-                near = gather_rows(mp[rows, cols], lambda r, c: cbuf[n, r // 2, pl.ds(4 * (r % 2) + c, 1), :], CROWS)
+                near = gather_rows(mp[rows, lines], lambda r, c: cbuf[n, r // 2, pl.ds(4 * (r % 2) + c, 1), :], CROWS)
                 for i in range(3):
                     for c in range(3):
-                        part = mx[3 * i + c, rows, cols] * near[c]
+                        part = mx[3 * i + c, rows, lines] * near[c]
                         sums[i] = part if sums[i] is None else sums[i] + part
             totals += [jnp.sum(s, axis=0, keepdims=True) for s in sums]
             totals.append(jnp.zeros((1, LANES), F32))
@@ -338,27 +387,35 @@
         value = gather_rows(
             idx_v[pl.ds(8 * t, 8), :], lambda r, c: cbuf[CSWEEPS - 1, r // 2, pl.ds(4 * (r % 2) + c, 1), :], CROWS
         )
-        rows = three(f2, hl2, hr2)
-        for n in range(8 if t == 0 else 4):
+        for n in range(8 * t, min(8 * t + 8, WIDE)):
             for c in range(3):
-                f3[pl.ds(c, 1), pl.ds((8 * t + n) * LANES, LANES)] = rows(c, 8 * t + n) + value[c][n : n + 1, :]
-    couple_fine(lambda c, n: f3[pl.ds(c, 1), pl.ds(n * LANES, LANES)])
-    f4[...] = KEEP * f3[:, pl.ds(WIN, NODE_DEV)] + s1_v[...] + w_v[...] * y_v[...]
-    send_halo(2, f4, hl4, hr4)
-
-    half = jnp.where(group_high == 0, last[0:4], last[4:8])
-    moved = half
+                f3[pl.ds(c, 1), cols(n)] = f2[pl.ds(c, 1), cols(n)] + value[c][n - 8 * t : n - 8 * t + 1, :]
+
+    def smooth(old, n, count):
+        here = cols(n - SIDE, count)
+        return KEEP * old[:, cols(n, count)] + f1[values, here] + f1[weights_at, here] * y_v[:, here]
+
+    couple_fine(border, lambda c, n: f3[pl.ds(c, 1), cols(n)])
+    for n in (SIDE, BLOCKS):
+        f4[:, cols(n, SIDE)] = smooth(f3, n, SIDE)
+    start_sides(2)
+    couple_fine(middle, lambda c, n: f3[pl.ds(c, 1), cols(n)])
+    f4[:, cols(2 * SIDE, BLOCKS - 2 * SIDE)] = smooth(f3, 2 * SIDE, BLOCKS - 2 * SIDE)
+    couple_fine(middle, lambda c, n: f4[pl.ds(c, 1), cols(n)])
+
+    part = jnp.where(group_high == 0, last[0:4], last[4:8])
+    moved = part
     for k in range(1, 4):
-        moved = jnp.where(group_low == k, pltpu.roll(half, LANES - 32 * k, 1), moved)
+        moved = jnp.where(group_low == k, pltpu.roll(part, LANES - 32 * k, 1), moved)
     cor_o[...] = moved[0:3, 0:AGG_DEV]
 
-    wait_halo(2, hl4, hr4)
-    couple_fine(three(f4, hl4, hr4))
-    sol_o[...] = KEEP * f4[...] + s1_v[...] + w_v[...] * y_v[...]
-
-    for n, from_left in enumerate((hl1, hl2, hl4)):
-        wait_bytes(from_left, halo_send.at[n, 0])
-        wait_bytes(from_left, halo_send.at[n, 1])
+    await_sides(2)
+    couple_fine(border, lambda c, n: f4[pl.ds(c, 1), cols(n)])
+    sol_o[...] = smooth(f4, SIDE, BLOCKS)
+
+    for n in range(3):
+        pl.when(has_right)(rightward[n].wait_send)
+        pl.when(has_left)(leftward[n].wait_send)
     for n, (ref, count) in enumerate(((far0, DEVICES), (rm, GROUPS), (far1, DEVICES))):
         wait_bytes(ref.at[pl.ds(0, count - 1)], far_send.at[n])
     for n in range(CSWEEPS - 1):
@@ -387,23 +444,17 @@
             pltpu.VMEM((3, AGG_DEV), F32),
             pltpu.VMEM((AGG_DEV, NNZ), I32),
             pltpu.VMEM((3, 3, AGG_DEV, NNZ), F32),
-            pltpu.VMEM((3, NODE_DEV), F32),
-            pltpu.VMEM((3, NODE_DEV), F32),
             pltpu.VMEM((32, NODE_DEV), I32),
             pltpu.VMEM((3, NODE_DEV), F32),
             pltpu.VMEM((8, NODE_DEV), F32),
             pltpu.VMEM((LANES, NODE_DEV), BF16),
             pltpu.VMEM((16, LANES), I32),
-            pltpu.VMEM((4, NODE_DEV), F32),
-            pltpu.VMEM((4, WIN), F32),
-            pltpu.VMEM((4, WIN), F32),
-            pltpu.VMEM((3, NODE_DEV), F32),
-            pltpu.VMEM((3, WIN), F32),
-            pltpu.VMEM((3, WIN), F32),
-            pltpu.VMEM((3, NODE_DEV + 2 * WIN), F32),
-            pltpu.VMEM((3, NODE_DEV), F32),
-            pltpu.VMEM((3, WIN), F32),
-            pltpu.VMEM((3, WIN), F32),
+            pltpu.VMEM((8, NODE_DEV), F32),
+            pltpu.VMEM((8, WIN), F32),
+            pltpu.VMEM((8, WIN), F32),
+            pltpu.VMEM((3, WIDE * LANES), F32),
+            pltpu.VMEM((3, WIDE * LANES), F32),
+            pltpu.VMEM((3, WIDE * LANES), F32),
             pltpu.VMEM((4, LANES), F32),
             pltpu.VMEM((DEVICES, 1, LANES), F32),
             pltpu.VMEM((DEVICES, 1, LANES), F32),
@@ -419,6 +470,7 @@
             dma((9,)),
             dma((3, 2)),
             dma((3, 2)),
+            pltpu.SemaphoreType.REGULAR,
             dma((3,)),
             dma((3,)),
             dma((CSWEEPS - 1,)),

time: 61.6 us -> 57.2 us (0.929)
  the two profiles are of different devices: /device:TPU:0 before, /device:TPU:1 now
where the time goes in v3:
time: 57.2 us; the launch traced here: 56.9 us
  Pallas kernels  53.7 us (94%)
  local copies, waits for them, and re-layouts  2.56 us (4%)
  between operations  0.64 us (1%)
    pallas_call x1, Pallas kernels, body(): pl.pallas_call(kernel, out_shape=(jax.ShapeDtypeStruct((3, NODE_DEV), F32...  53.7 us
    unnamed x2, local copies, waits for them, and re-layouts  2.56 us

profile of v3, /device:TPU:1, one launch (start us, length us, event | category | flops | bytes accessed | tf_op | source)
XLA Modules:
  0.0 56.9 jit_solution(430299464586038719)
XLA Ops:
  0.6 53.7 %vcycle.1 = (f32[3,1024]{1,0:T(4,128)}, f32[3,32]{1,0:T(4,128)}) custom-call(f32[3,1024]{1,0:T(4,128)} %bitcast.13, f32[3,1024]{1,0:T(4,128)} %bitcast.14, s32[27,1024]{1,0:T(8,128)} %bitcast.12, f32[3,3,27,1024]{3,2,1,0:T(8,128)} %bitcast.10, s32[8,128]{1,0:T(8,128)} %bitcast.16, s32[1,32]{1,0:T(1,128)} %bitcast.19, f32[3,32]{1,0:T(4,128)} %bitcast.17, ...), custom_call_target="tpu_custom_call" | custom-call | tf_op jit(solution)/shard_map/vcycle/pallas_call | solution.py:429
  54.3 1.3 %copy.13 = f32[1024,3]{0,1:T(4,128)} copy(f32[1024,3]{0,1:T(4,128)} %bitcast.15) | data formatting | bytes 24576
  55.6 1.2 %copy.14 = f32[32,3]{0,1:T(4,128)} copy(f32[32,3]{0,1:T(4,128)} %bitcast.18) | data formatting | bytes 768

commit v4 on v3

--- a/solution.py
+++ b/solution.py
@@ -140,8 +140,6 @@
     f1[pl.ds(4, 3), :] = w0
     for n in range(BLOCKS):
         f1[pl.ds(3, 1), cols(n)] = node_place[n : n + 1, :]
-    for n in range(4, 9):
-        loads[n].wait()
     pl.semaphore_wait(barrier, CUBE - 1 + GROUPS - 1 + 2)
 
     def to_right(n, src, dst):
@@ -182,6 +180,8 @@
     for peer in group_peers:
         pl.semaphore_signal(entered, inc=1, device_id=(peer,), device_id_type=MESH)
 
+    for n in range(4, 9):
+        loads[n].wait()
     stage[pl.ds(0, 3), pl.ds(0, AGG_DEV)] = cd_v[...]
     own = stage[...]
     line = own[0:1]
@@ -208,10 +208,6 @@
                     whole = moved if j == 0 else jnp.where((lane // 32) == j, moved, whole)
                 table[c, pl.ds(8 * t, 8), :] = whole
 
-    def send_cube(ref, send_sem, recv_sem):
-        for peer in cube_peers:
-            send(ref.at[member], ref.at[member], send_sem, recv_sem, peer)
-
     def number_columns(n, carry):
         here = pl.ds(pl.multiple_of(n * LANES, LANES), LANES)
         q_s[pl.ds(24, 8), here] = jnp.zeros((8, LANES), I32)
@@ -227,9 +223,16 @@
     pack[2, pl.ds(32, 32), pl.ds(0, NNZ)] = position_of(cq_v[...]).astype(F32)
     for n in range(3):
         rm[group, pl.ds(32 * n, 32), :] = pack[n].T[0:32, :]
-    send_group(1, rm)
 
     lax.fori_loop(0, BLOCKS, number_columns, 0)
+
+    def label_block(n, carry):
+        label = lax.broadcasted_iota(I32, (LANES, LANES), 0) % AGG_DEV
+        hit = agg_v[pl.ds(n, 1), :] == label
+        onehot[:, pl.ds(pl.multiple_of(n * LANES, LANES), LANES)] = hit.astype(F32).astype(BF16)
+        return carry
+
+    lax.fori_loop(0, BLOCKS, label_block, 0)
 
     def couple_fine(blocks, field):
         for n in blocks:
@@ -268,23 +271,17 @@
     values, weights_at = pl.ds(0, 3), pl.ds(4, 3)
 
     couple_fine(middle, start_field)
-    pl.semaphore_wait(entered, GROUPS - 1)
-    send_all(0, far0)
 
     await_sides(0)
     couple_fine(border, start_field)
     inside = cols(SIDE, BLOCKS)
     f2[:, inside] = (1.0 + KEEP) * f1[values, :] + f1[weights_at, :] * y_v[...]
     start_sides(1)
+    pl.semaphore_wait(entered, GROUPS - 1)
+    send_all(0, far0)
+    send_group(1, rm)
     couple_fine(middle, lambda c, n: f2[pl.ds(c, 1), cols(n)])
 
-    def label_block(n, carry):
-        label = lax.broadcasted_iota(I32, (LANES, LANES), 0) % AGG_DEV
-        hit = agg_v[pl.ds(n, 1), :] == label
-        onehot[:, pl.ds(pl.multiple_of(n * LANES, LANES), LANES)] = hit.astype(F32).astype(BF16)
-        return carry
-
-    lax.fori_loop(0, BLOCKS, label_block, 0)
     r_v[...] = jnp.zeros_like(r_v)
     await_sides(1)
     couple_fine(border, lambda c, n: f2[pl.ds(c, 1), cols(n)])
@@ -361,35 +358,60 @@
     first = jnp.where(unused, 0.0, cbuf[0, member])
     weight = jnp.where(unused, 0.0, wbuf[member])
 
-    def sweep(n, current):
+    def place(k):
+        slot = member
+        for p, w in enumerate((1, 2, 4, 8)):
+            if (k >> p) & 1:
+                slot = slot + (1 - 2 * ((member // w) % 2)) * w
+        return slot
+
+    stages = [[k for k in range(CUBE) if bin(k >> 1).count("1") == hops] for hops in range(4)]
+
+    def coarse_values(n, places, arrive):
+        found = [[jnp.zeros((8, LANES), F32)] * 3 for _ in places]
+        for stage_of in stages:
+            for k in stage_of:
+                if k and arrive:
+                    there = cbuf.at[n, place(k)]
+                    pltpu.make_async_copy(there, there, sweep_recv.at[n - 1, k]).wait()
+            for t, where in enumerate(places):
+                high, low = where() >> 7, where() & 127
+                for k in stage_of:
+                    slot = place(k)
+                    for h in range(2):
+                        hit = high == slot * 2 + h
+                        for c in range(3):
+                            taken = pick(cbuf[n, slot, pl.ds(4 * h + c, 1), :], low)
+                            found[t][c] = jnp.where(hit, taken, found[t][c])
+        return found
+
+    tiles = [(pl.ds(8 * k, 8), pl.ds(LANES * h, LANES)) for h in range(2) for k in range(4)]
+
+    def sweep(n, current, arrive):
+        near = coarse_values(n, [lambda at=at: mp[at] for at in tiles], arrive)
         totals = []
         for h in range(2):
-            lines = pl.ds(LANES * h, LANES)
             sums = [None] * 3
-            for k in range(4):
-                rows = pl.ds(8 * k, 8)
-                near = gather_rows(mp[rows, lines], lambda r, c: cbuf[n, r // 2, pl.ds(4 * (r % 2) + c, 1), :], CROWS)
+            for t in range(4 * h, 4 * h + 4):
                 for i in range(3):
                     for c in range(3):
-                        part = mx[3 * i + c, rows, lines] * near[c]
+                        part = mx[3 * i + c, tiles[t][0], tiles[t][1]] * near[t][c]
                         sums[i] = part if sums[i] is None else sums[i] + part
             totals += [jnp.sum(s, axis=0, keepdims=True) for s in sums]
             totals.append(jnp.zeros((1, LANES), F32))
         current = KEEP * current + first + weight * jnp.concatenate(totals, axis=0)
         cbuf[n + 1, member] = current
-        send_cube(cbuf.at[n + 1], sweep_send.at[n], sweep_recv.at[n])
-        wait_bytes(cbuf.at[n + 1, pl.ds(0, CUBE - 1)], sweep_recv.at[n])
+        mine = cbuf.at[n + 1, member]
+        for k in reversed(range(1, CUBE)):
+            send(mine, mine, sweep_send.at[n], sweep_recv.at[n, k], cube_peers[k - 1])
         return current
 
-    last = lax.fori_loop(0, CSWEEPS - 1, sweep, first)
-
-    for t in range(2):
-        value = gather_rows(
-            idx_v[pl.ds(8 * t, 8), :], lambda r, c: cbuf[CSWEEPS - 1, r // 2, pl.ds(4 * (r % 2) + c, 1), :], CROWS
-        )
-        for n in range(8 * t, min(8 * t + 8, WIDE)):
-            for c in range(3):
-                f3[pl.ds(c, 1), cols(n)] = f2[pl.ds(c, 1), cols(n)] + value[c][n - 8 * t : n - 8 * t + 1, :]
+    last = lax.fori_loop(1, CSWEEPS - 1, lambda n, current: sweep(n, current, True), sweep(0, first, False))
+
+    found = coarse_values(CSWEEPS - 1, [lambda t=t: idx_v[pl.ds(8 * t, 8), :] for t in range(2)], True)
+    for n in range(WIDE):
+        for c in range(3):
+            f3[pl.ds(c, 1), cols(n)] = f2[pl.ds(c, 1), cols(n)] + found[n // 8][c][n % 8 : n % 8 + 1, :]
 
     def smooth(old, n, count):
         here = cols(n - SIDE, count)
@@ -474,7 +496,7 @@
             dma((3,)),
             dma((3,)),
             dma((CSWEEPS - 1,)),
-            dma((CSWEEPS - 1,)),
+            dma((CSWEEPS - 1, CUBE)),
         ],
         compiler_params=pltpu.CompilerParams(collective_id=0, has_side_effects=True),
         name="vcycle",

time: 57.2 us -> 54.7 us (0.956)
  Pallas kernels: 53.7 us -> 51.2 us
    pallas_call x1, Pallas kernels: 53.7 us -> 51.2 us  [body(): pl.pallas_call(kernel, out_shape=(jax.ShapeDtypeStruct((3, NODE_DEV), F32...]
where the time goes in v4:
time: 54.7 us; the launch traced here: 54.4 us
  Pallas kernels  51.2 us (94%)
  local copies, waits for them, and re-layouts  2.56 us (5%)
  between operations  0.64 us (1%)
    pallas_call x1, Pallas kernels, body(): pl.pallas_call(kernel, out_shape=(jax.ShapeDtypeStruct((3, NODE_DEV), F32...  51.2 us
    unnamed x2, local copies, waits for them, and re-layouts  2.56 us

profile of v4, /device:TPU:1, one launch (start us, length us, event | category | flops | bytes accessed | tf_op | source)
XLA Modules:
  0.0 54.4 jit_solution(2993028998521497674)
XLA Ops:
  0.6 51.2 %vcycle.1 = (f32[3,1024]{1,0:T(4,128)}, f32[3,32]{1,0:T(4,128)}) custom-call(f32[3,1024]{1,0:T(4,128)} %bitcast.13, f32[3,1024]{1,0:T(4,128)} %bitcast.14, s32[27,1024]{1,0:T(8,128)} %bitcast.12, f32[3,3,27,1024]{3,2,1,0:T(8,128)} %bitcast.10, s32[8,128]{1,0:T(8,128)} %bitcast.16, s32[1,32]{1,0:T(1,128)} %bitcast.19, f32[3,32]{1,0:T(4,128)} %bitcast.17, ...), custom_call_target="tpu_custom_call" | custom-call | tf_op jit(solution)/shard_map/vcycle/pallas_call | solution.py:451
  51.8 1.3 %copy.13 = f32[1024,3]{0,1:T(4,128)} copy(f32[1024,3]{0,1:T(4,128)} %bitcast.15) | data formatting | bytes 24576
  53.1 1.2 %copy.14 = f32[32,3]{0,1:T(4,128)} copy(f32[32,3]{0,1:T(4,128)} %bitcast.18) | data formatting | bytes 768

commit v5 on v4

--- a/solution.py
+++ b/solution.py
@@ -57,7 +57,7 @@
 
 def kernel(
     b_h, d_h, q_h, a_h, agg_h, row_h, cd_h, cq_h, ca_h,
-    sol_o, cor_o,
+    out_o,
     b_v, d_v, q_v, a_v, agg_v, row_v, cd_v, cq_v, ca_v,
  q_s, y_v, r_v, onehot, idx_v,
     f1, f1l, f1r, f2, f3, f4,
@@ -429,11 +429,11 @@
     moved = part
     for k in range(1, 4):
         moved = jnp.where(group_low == k, pltpu.roll(part, LANES - 32 * k, 1), moved)
-    cor_o[...] = moved[0:3, 0:AGG_DEV]
+    out_o[:, pl.ds(NODE_DEV, LANES)] = moved[0:3]
 
     await_sides(2)
     couple_fine(border, lambda c, n: f4[pl.ds(c, 1), cols(n)])
-    sol_o[...] = smooth(f4, SIDE, BLOCKS)
+    out_o[:, pl.ds(0, NODE_DEV)] = smooth(f4, SIDE, BLOCKS)
 
     for n in range(3):
         pl.when(has_right)(rightward[n].wait_send)
@@ -444,18 +444,20 @@
         wait_bytes(cbuf.at[n + 1, pl.ds(0, CUBE - 1)], sweep_send.at[n])
 
 
+def split(all_ref, sol_o, cor_o):
+    sol_o[...] = all_ref[:, pl.ds(0, NODE_DEV)]
+    cor_o[...] = all_ref[:, pl.ds(NODE_DEV, LANES)][:, 0:AGG_DEV]
+
+
 def body(b, d, q, a, agg, row, cd, cq, ca):
     any_spec = pl.BlockSpec(memory_space=pl.ANY)
     vmem = pl.BlockSpec(memory_space=pltpu.VMEM)
     dma = pltpu.SemaphoreType.DMA
-    sol, cor = pl.pallas_call(
+    out = pl.pallas_call(
         kernel,
-        out_shape=(
-            jax.ShapeDtypeStruct((3, NODE_DEV), F32),
-            jax.ShapeDtypeStruct((3, AGG_DEV), F32),
-        ),
+        out_shape=pltpu.VMEM((3, NODE_DEV + LANES), F32),
         in_specs=[any_spec] * 9,
-        out_specs=(vmem, vmem),
+        out_specs=vmem,
         scratch_shapes=[
             pltpu.VMEM((3, NODE_DEV), F32),
             pltpu.VMEM((3, NODE_DEV), F32),
@@ -511,6 +513,16 @@
         cq,
         ca.transpose(2, 3, 0, 1),
     )
+    sol, cor = pl.pallas_call(
+        split,
+        out_shape=(
+            jax.ShapeDtypeStruct((3, NODE_DEV), F32),
+            jax.ShapeDtypeStruct((3, AGG_DEV), F32),
+        ),
+        in_specs=[vmem],
+        out_specs=(vmem, vmem),
+        name="split",
+    )(pltpu.with_memory_space_constraint(out, pltpu.VMEM))
     return sol.T, cor.T
 
 

time: 54.7 us -> 52 us (0.951)
  local copies, waits for them, and re-layouts: 2.56 us -> 0 us
    unnamed x2 -> x0, local copies, waits for them, and re-layouts: 2.56 us -> none
    pallas_call x1 -> x2, Pallas kernels: 51.2 us -> 51.2 us  [the longest x1 50.5 us: body(): pl.pallas_call(kernel, out_shape=pltpu.VMEM((3, NODE_DEV + LANES), F32),...]
where the time goes in v5:
time: 52 us; the launch traced here: 51.8 us
  Pallas kernels  51.2 us (98%)
  between operations  0.64 us (1%)
    pallas_call x1, Pallas kernels, body(): pl.pallas_call(kernel, out_shape=pltpu.VMEM((3, NODE_DEV + LANES), F32),...  50.5 us

profile of v5, /device:TPU:1, one launch (start us, length us, event | category | flops | bytes accessed | tf_op | source)
XLA Modules:
  0.0 51.8 jit_solution(9814822690170232381)
XLA Ops:
  0.6 50.5 %vcycle.1.all_ref = f32[3,1152]{1,0:T(4,128)S(1)} custom-call(f32[3,1024]{1,0:T(4,128)} %bitcast.13, f32[3,1024]{1,0:T(4,128)} %bitcast.14, s32[27,1024]{1,0:T(8,128)} %bitcast.12, f32[3,3,27,1024]{3,2,1,0:T(8,128)} %bitcast.10, s32[8,128]{1,0:T(8,128)} %bitcast.15, s32[1,32]{1,0:T(1,128)} %bitcast.17, f32[3,32]{1,0:T(4,128)} %bitcast.16, s32[32,27]{1,0:T(8,128)} %cq_h.1, ...), custom_call_target="tpu_custom_call" | custom-call | tf_op jit(solution)/shard_map/vcycle/pallas_call | solution.py:456
  51.2 0.6 %split.1 = (f32[3,1024]{1,0:T(4,128)}, f32[3,32]{1,0:T(4,128)}) custom-call(f32[3,1152]{1,0:T(4,128)S(1)} %vcycle.1.all_ref), custom_call_target="tpu_custom_call" | custom-call | tf_op jit(solution)/shard_map/split/pallas_call | solution.py:516

commit v6 on v5

--- a/solution.py
+++ b/solution.py
@@ -112,7 +112,8 @@
         loads.append(copy)
 
     barrier = pltpu.get_barrier_semaphore()
-    for peer in cube_peers + group_peers + [left, right]:
+    beside = [group_peers[k - 1] for k in (1, 2, 4)]
+    for peer in cube_peers + beside + [left, right]:
         pl.semaphore_signal(barrier, inc=1, device_id=(peer,), device_id_type=MESH)
 
     def send(src, dst, send_sem, recv_sem, peer):
@@ -140,7 +141,7 @@
     f1[pl.ds(4, 3), :] = w0
     for n in range(BLOCKS):
         f1[pl.ds(3, 1), cols(n)] = node_place[n : n + 1, :]
-    pl.semaphore_wait(barrier, CUBE - 1 + GROUPS - 1 + 2)
+    pl.semaphore_wait(barrier, CUBE - 1 + 3 + 2)
 
     def to_right(n, src, dst):
         return pltpu.make_async_remote_copy(
@@ -177,8 +178,11 @@
         pl.when(has_right)(leftward[n].wait_recv)
 
     start_sides(0)
-    for peer in group_peers:
-        pl.semaphore_signal(entered, inc=1, device_id=(peer,), device_id_type=MESH)
+
+    def tell(n):
+        pl.semaphore_signal(entered.at[n], inc=1, device_id=(beside[n],), device_id_type=MESH)
+
+    tell(0)
 
     for n in range(4, 9):
         loads[n].wait()
@@ -270,14 +274,18 @@
     border = [*range(SIDE, 2 * SIDE), *range(BLOCKS, BLOCKS + SIDE)]
     values, weights_at = pl.ds(0, 3), pl.ds(4, 3)
 
+    pl.semaphore_wait(entered.at[0], 1)
+    tell(1)
     couple_fine(middle, start_field)
+    pl.semaphore_wait(entered.at[1], 1)
+    tell(2)
 
     await_sides(0)
     couple_fine(border, start_field)
     inside = cols(SIDE, BLOCKS)
     f2[:, inside] = (1.0 + KEEP) * f1[values, :] + f1[weights_at, :] * y_v[...]
     start_sides(1)
-    pl.semaphore_wait(entered, GROUPS - 1)
+    pl.semaphore_wait(entered.at[2], 1)
     send_all(0, far0)
     send_group(1, rm)
     couple_fine(middle, lambda c, n: f2[pl.ds(c, 1), cols(n)])
@@ -322,6 +330,7 @@
         for c in range(3):
             wbuf[r // 2, pl.ds(4 * (r % 2) + c, 1), :] = tab0[c, pl.ds(r, 1), :]
     wait_bytes(rm.at[pl.ds(0, GROUPS - 1)], far_recv.at[1])
+    spare = {}
     for h in range(2):
         for e4 in range(3):
             for k in range(4):
@@ -335,6 +344,12 @@
                         moved = parts[j] if j == s else pltpu.roll(parts[j], 32 * ((j - s) % 4), 1)
                         whole = moved if j == 0 else jnp.where((lane // 32) == j, moved, whole)
                     rows, lines = pl.ds(8 * k, 8), pl.ds(LANES * h, LANES)
+                    if k == 3:
+                        lines = pl.ds(0, LANES)
+                        if h == 0:
+                            spare[e] = whole
+                            continue
+                        whole = spare[e] + pltpu.roll(whole, NNZ - 24, 0)
                     if e < 9:
                         mx[e, rows, lines] = whole
                     else:
@@ -385,19 +400,28 @@
                             found[t][c] = jnp.where(hit, taken, found[t][c])
         return found
 
-    tiles = [(pl.ds(8 * k, 8), pl.ds(LANES * h, LANES)) for h in range(2) for k in range(4)]
+    tiles = [(pl.ds(8 * k, 8), pl.ds(LANES * h, LANES)) for h in range(2) for k in range(3)]
+    tiles.append((pl.ds(24, 8), pl.ds(0, LANES)))
+    sublane = lax.broadcasted_iota(I32, (8, LANES), 0)
 
     def sweep(n, current, arrive):
         near = coarse_values(n, [lambda at=at: mp[at] for at in tiles], arrive)
+
+        def product(i, which):
+            total = None
+            for t in which:
+                for c in range(3):
+                    part = mx[3 * i + c, tiles[t][0], tiles[t][1]] * near[t][c]
+                    total = part if total is None else total + part
+            return total
+
+        shared = [product(i, (6,)) for i in range(3)]
         totals = []
         for h in range(2):
-            sums = [None] * 3
-            for t in range(4 * h, 4 * h + 4):
-                for i in range(3):
-                    for c in range(3):
-                        part = mx[3 * i + c, tiles[t][0], tiles[t][1]] * near[t][c]
-                        sums[i] = part if sums[i] is None else sums[i] + part
-            totals += [jnp.sum(s, axis=0, keepdims=True) for s in sums]
+            for i in range(3):
+                mine = sublane < NNZ - 24 if h == 0 else sublane >= NNZ - 24
+                total = product(i, range(3 * h, 3 * h + 3)) + jnp.where(mine, shared[i], 0.0)
+                totals.append(jnp.sum(total, axis=0, keepdims=True))
             totals.append(jnp.zeros((1, LANES), F32))
         current = KEEP * current + first + weight * jnp.concatenate(totals, axis=0)
         cbuf[n + 1, member] = current
@@ -494,7 +518,7 @@
             dma((9,)),
             dma((3, 2)),
             dma((3, 2)),
-            pltpu.SemaphoreType.REGULAR,
+            pltpu.SemaphoreType.REGULAR((3,)),
             dma((3,)),
             dma((3,)),
             dma((CSWEEPS - 1,)),

time: 52 us -> 51.1 us (0.983)
  Pallas kernels: 51.2 us -> 50.2 us
    pallas_call x1, Pallas kernels: 50.5 us -> 49.6 us  [body(): pl.pallas_call(kernel, out_shape=pltpu.VMEM((3, NODE_DEV + LANES), F32),...]
where the time goes in v6:
time: 51.1 us; the launch traced here: 50.9 us
  Pallas kernels  50.2 us (98%)
  between operations  0.64 us (1%)
    pallas_call x1, Pallas kernels, body(): pl.pallas_call(kernel, out_shape=pltpu.VMEM((3, NODE_DEV + LANES), F32),...  49.6 us

profile of v6, /device:TPU:1, one launch (start us, length us, event | category | flops | bytes accessed | tf_op | source)
XLA Modules:
  0.0 50.9 jit_solution(11091279642242578170)
XLA Ops:
  0.6 49.6 %vcycle.1.all_ref = f32[3,1152]{1,0:T(4,128)S(1)} custom-call(f32[3,1024]{1,0:T(4,128)} %bitcast.13, f32[3,1024]{1,0:T(4,128)} %bitcast.14, s32[27,1024]{1,0:T(8,128)} %bitcast.12, f32[3,3,27,1024]{3,2,1,0:T(8,128)} %bitcast.10, s32[8,128]{1,0:T(8,128)} %bitcast.15, s32[1,32]{1,0:T(1,128)} %bitcast.17, f32[3,32]{1,0:T(4,128)} %bitcast.16, s32[32,27]{1,0:T(8,128)} %cq_h.1, ...), custom_call_target="tpu_custom_call" | custom-call | tf_op jit(solution)/shard_map/vcycle/pallas_call | solution.py:480
  50.3 0.6 %split.1 = (f32[3,1024]{1,0:T(4,128)}, f32[3,32]{1,0:T(4,128)}) custom-call(f32[3,1152]{1,0:T(4,128)S(1)} %vcycle.1.all_ref), custom_call_target="tpu_custom_call" | custom-call | tf_op jit(solution)/shard_map/split/pallas_call | solution.py:540

commit v7 on v6

--- a/solution.py
+++ b/solution.py
@@ -64,7 +64,7 @@
     stage, far0, far1, tab0, tab1,
     pack, rm, mx, mp,
     inv_v, wbuf, cbuf,
-    load_sem, side_send, side_recv, entered, far_send, far_recv, sweep_send, sweep_recv,
+    load_sem, side_send, side_recv, entered, far_send, far_recv, pair_send, pair_recv, sweep_send, sweep_recv,
 ):
     me = lax.axis_index("dom")
 
@@ -90,12 +90,14 @@
 
     along_x, along_z, along_y = ring(1, 2), ring(3, 4), ring(5, 6)
     cores = [bit(0), 1 - bit(0)]
-    steps = [(x, z, y, c) for x in range(4) for z in range(4) for y in range(4) for c in range(2)]
+    steps = [(x, z, y) for x in range(4) for z in range(4) for y in range(4)]
     hops = (0, 1, 2, 1)
-    steps = sorted(steps, key=lambda v: -(hops[v[0]] + hops[v[1]] + hops[v[2]]) - 0.5 * v[3])
-    all_peers = [along_x[x] + along_z[z] + along_y[y] + cores[c] for x, z, y, c in steps if (x, z, y, c) != (0, 0, 0, 0)]
+    steps = sorted(steps, key=lambda v: -(hops[v[0]] + hops[v[1]] + hops[v[2]]))
+    all_peers = [along_x[x] + along_z[z] + along_y[y] + cores[0] for x, z, y in steps if (x, z, y) != (0, 0, 0)]
     my_high = member * 2 + bit(6)
-    my_slot = ((my_high // 8) * 4 + group_low) * 8 + my_high % 8
+    pair = ((my_high // 8) * 4 + group_low) * 8 + (my_high % 8 // 4) * 4 + bit(6) * 2
+    my_slot = pair + bit(0)
+    partner = along_x[0] + along_z[0] + along_y[0] + cores[1]
     cube_peers = [flipped(CUBE_BITS, k) for k in range(1, CUBE)]
     group_peers = [flipped(GROUP_BITS, k) for k in range(1, GROUPS)]
     left, right = (me + DEVICES - 1) % DEVICES, (me + 1) % DEVICES
@@ -169,15 +171,31 @@
     ]
     has_left, has_right = me > 0, me < DEVICES - 1
 
-    def start_sides(n):
-        pl.when(has_right)(rightward[n].start)
-        pl.when(has_left)(leftward[n].start)
-
-    def await_sides(n):
-        pl.when(has_left)(rightward[n].wait_recv)
-        pl.when(has_right)(leftward[n].wait_recv)
-
-    start_sides(0)
+    def start_side(n, side):
+        if side == "left":
+            pl.when(has_left)(leftward[n].start)
+        else:
+            pl.when(has_right)(rightward[n].start)
+
+    def await_side(n, side):
+        if side == "left":
+            pl.when(has_left)(rightward[n].wait_recv)
+        else:
+            pl.when(has_right)(leftward[n].wait_recv)
+
+    def each_side(act, chip_first):
+        @pl.when(bit(0) == 0)
+        def _():
+            for side in ("right", "left") if chip_first else ("left", "right"):
+                act(side)
+
+        @pl.when(bit(0) == 1)
+        def _():
+            for side in ("left", "right") if chip_first else ("right", "left"):
+                act(side)
+
+    start_side(0, "left")
+    start_side(0, "right")
 
     def tell(n):
         pl.semaphore_signal(entered.at[n], inc=1, device_id=(beside[n],), device_id_type=MESH)
@@ -197,14 +215,20 @@
         for peer in group_peers:
             send(ref.at[group], ref.at[group], far_send.at[n], far_recv.at[n], peer)
 
+    def send_partner(n, ref):
+        send(ref.at[my_slot], ref.at[my_slot], pair_send.at[n], pair_recv.at[n], partner)
+
     def send_all(n, ref):
+        wait_bytes(ref.at[pl.ds(0, 1)], pair_recv.at[n])
+        both = ref.at[pl.ds(pair, 2)]
         for peer in all_peers:
-            send(ref.at[my_slot], ref.at[my_slot], far_send.at[n], far_recv.at[n], peer)
+            send(both, both, far_send.at[n], far_recv.at[n], peer)
 
     def receive_all(n, ref, table):
-        wait_bytes(ref.at[pl.ds(0, DEVICES - 1)], far_recv.at[n])
+        wait_bytes(ref.at[pl.ds(0, DEVICES - 2)], far_recv.at[n])
+        order = [4 * (r // 4) + 2 * (r % 2) + r // 2 % 2 for r in range(8)]
         for t in range(4):
-            parts = [ref[pl.ds(32 * t + 8 * j, 8), 0, :] for j in range(4)]
+            parts = [jnp.concatenate([ref[32 * t + 8 * j + r] for r in order], axis=0) for j in range(4)]
             for c in range(table.shape[0]):
                 whole = None
                 for j in range(4):
@@ -222,6 +246,7 @@
         pack[e // 4, pl.ds(pl.multiple_of(32 * (e % 4), 32), 32), pl.ds(0, NNZ)] = ca_v[e // 3, e % 3]
         return carry
 
+    send_partner(0, far0)
     pack[...] = jnp.zeros_like(pack)
     lax.fori_loop(0, 9, pack_one, 0)
     pack[2, pl.ds(32, 32), pl.ds(0, NNZ)] = position_of(cq_v[...]).astype(F32)
@@ -271,28 +296,40 @@
         return first_field(pl.ds(c, 1), n)
 
     middle = range(2 * SIDE, BLOCKS)
-    border = [*range(SIDE, 2 * SIDE), *range(BLOCKS, BLOCKS + SIDE)]
+    border = {"left": range(SIDE, 2 * SIDE), "right": range(BLOCKS, BLOCKS + SIDE)}
     values, weights_at = pl.ds(0, 3), pl.ds(4, 3)
 
     pl.semaphore_wait(entered.at[0], 1)
     tell(1)
     couple_fine(middle, start_field)
+    inside = cols(SIDE, BLOCKS)
+
+    def second(blocks):
+        here, count = cols(blocks[0] - SIDE, len(blocks)), len(blocks)
+        f2[:, cols(blocks[0], count)] = (1.0 + KEEP) * f1[values, here] + f1[weights_at, here] * y_v[:, here]
+
+    second(middle)
     pl.semaphore_wait(entered.at[1], 1)
     tell(2)
 
-    await_sides(0)
-    couple_fine(border, start_field)
-    inside = cols(SIDE, BLOCKS)
-    f2[:, inside] = (1.0 + KEEP) * f1[values, :] + f1[weights_at, :] * y_v[...]
-    start_sides(1)
+    def first_apply(side):
+        await_side(0, side)
+        couple_fine(border[side], start_field)
+        second(border[side])
+        start_side(1, side)
+
+    each_side(first_apply, True)
     pl.semaphore_wait(entered.at[2], 1)
     send_all(0, far0)
     send_group(1, rm)
     couple_fine(middle, lambda c, n: f2[pl.ds(c, 1), cols(n)])
 
     r_v[...] = jnp.zeros_like(r_v)
-    await_sides(1)
-    couple_fine(border, lambda c, n: f2[pl.ds(c, 1), cols(n)])
+    def second_apply(side):
+        await_side(1, side)
+        couple_fine(border[side], lambda c, n: f2[pl.ds(c, 1), cols(n)])
+
+    each_side(second_apply, True)
     r_v[pl.ds(0, 3), :] = b_v[...] - d_v[...] * f2[:, inside] + y_v[...]
     rest = r_v[...]
     p0 = rest.astype(BF16).astype(F32)
@@ -305,6 +342,7 @@
     for n in range(1, 3):
         line = jnp.where(lane // AGG_DEV == n, sums[n : n + 1], line)
     far1[my_slot] = line
+    send_partner(2, far1)
     send_all(2, far1)
 
     receive_all(0, far0, tab0)
@@ -441,10 +479,12 @@
         here = cols(n - SIDE, count)
         return KEEP * old[:, cols(n, count)] + f1[values, here] + f1[weights_at, here] * y_v[:, here]
 
-    couple_fine(border, lambda c, n: f3[pl.ds(c, 1), cols(n)])
-    for n in (SIDE, BLOCKS):
-        f4[:, cols(n, SIDE)] = smooth(f3, n, SIDE)
-    start_sides(2)
+    def third_apply(side):
+        couple_fine(border[side], lambda c, n: f3[pl.ds(c, 1), cols(n)])
+        f4[:, cols(border[side][0], SIDE)] = smooth(f3, border[side][0], SIDE)
+        start_side(2, side)
+
+    each_side(third_apply, False)
     couple_fine(middle, lambda c, n: f3[pl.ds(c, 1), cols(n)])
     f4[:, cols(2 * SIDE, BLOCKS - 2 * SIDE)] = smooth(f3, 2 * SIDE, BLOCKS - 2 * SIDE)
     couple_fine(middle, lambda c, n: f4[pl.ds(c, 1), cols(n)])
@@ -455,15 +495,20 @@
         moved = jnp.where(group_low == k, pltpu.roll(part, LANES - 32 * k, 1), moved)
     out_o[:, pl.ds(NODE_DEV, LANES)] = moved[0:3]
 
-    await_sides(2)
-    couple_fine(border, lambda c, n: f4[pl.ds(c, 1), cols(n)])
+    def last_apply(side):
+        await_side(2, side)
+        couple_fine(border[side], lambda c, n: f4[pl.ds(c, 1), cols(n)])
+
+    each_side(last_apply, True)
     out_o[:, pl.ds(0, NODE_DEV)] = smooth(f4, SIDE, BLOCKS)
 
     for n in range(3):
         pl.when(has_right)(rightward[n].wait_send)
         pl.when(has_left)(leftward[n].wait_send)
-    for n, (ref, count) in enumerate(((far0, DEVICES), (rm, GROUPS), (far1, DEVICES))):
+    for n, (ref, count) in enumerate(((far0, DEVICES - 1), (rm, GROUPS), (far1, DEVICES - 1))):
         wait_bytes(ref.at[pl.ds(0, count - 1)], far_send.at[n])
+        if n != 1:
+            wait_bytes(ref.at[pl.ds(0, 1)], pair_send.at[n])
     for n in range(CSWEEPS - 1):
         wait_bytes(cbuf.at[n + 1, pl.ds(0, CUBE - 1)], sweep_send.at[n])
 
@@ -521,6 +566,8 @@
             pltpu.SemaphoreType.REGULAR((3,)),
             dma((3,)),
             dma((3,)),
+            dma((3,)),
+            dma((3,)),
             dma((CSWEEPS - 1,)),
             dma((CSWEEPS - 1, CUBE)),
         ],

time: 51.1 us -> 50 us (0.978)
  Pallas kernels: 50.2 us -> 49.1 us
    pallas_call x1, Pallas kernels: 49.6 us -> 48.5 us  [body(): pl.pallas_call(kernel, out_shape=pltpu.VMEM((3, NODE_DEV + LANES), F32),...]
where the time goes in v7:
time: 50 us; the launch traced here: 49.8 us
  Pallas kernels  49.1 us (98%)
  between operations  0.64 us (1%)
    pallas_call x1, Pallas kernels, body(): pl.pallas_call(kernel, out_shape=pltpu.VMEM((3, NODE_DEV + LANES), F32),...  48.5 us

profile of v7, /device:TPU:1, one launch (start us, length us, event | category | flops | bytes accessed | tf_op | source)
XLA Modules:
  0.0 49.8 jit_solution(4052499197844457156)
XLA Ops:
  0.6 48.5 %vcycle.1.all_ref = f32[3,1152]{1,0:T(4,128)S(1)} custom-call(f32[3,1024]{1,0:T(4,128)} %bitcast.13, f32[3,1024]{1,0:T(4,128)} %bitcast.14, s32[27,1024]{1,0:T(8,128)} %bitcast.12, f32[3,3,27,1024]{3,2,1,0:T(8,128)} %bitcast.10, s32[8,128]{1,0:T(8,128)} %bitcast.15, s32[1,32]{1,0:T(1,128)} %bitcast.17, f32[3,32]{1,0:T(4,128)} %bitcast.16, s32[32,27]{1,0:T(8,128)} %cq_h.1, ...), custom_call_target="tpu_custom_call" | custom-call | tf_op jit(solution)/shard_map/vcycle/pallas_call | solution.py:525
  49.2 0.6 %split.1 = (f32[3,1024]{1,0:T(4,128)}, f32[3,32]{1,0:T(4,128)}) custom-call(f32[3,1152]{1,0:T(4,128)S(1)} %vcycle.1.all_ref), custom_call_target="tpu_custom_call" | custom-call | tf_op jit(solution)/shard_map/split/pallas_call | solution.py:587

commit v8 on v7

--- a/solution.py
+++ b/solution.py
@@ -319,10 +319,10 @@
         start_side(1, side)
 
     each_side(first_apply, True)
+    couple_fine(middle, lambda c, n: f2[pl.ds(c, 1), cols(n)])
     pl.semaphore_wait(entered.at[2], 1)
     send_all(0, far0)
     send_group(1, rm)
-    couple_fine(middle, lambda c, n: f2[pl.ds(c, 1), cols(n)])
 
     r_v[...] = jnp.zeros_like(r_v)
     def second_apply(side):

time: 50 us -> 50 us (level)
  no operation moved by 1% of the time
where the time goes in v8:
time: 50 us; the launch traced here: 49.8 us
  Pallas kernels  49.2 us (98%)
  between operations  0.64 us (1%)
    pallas_call x1, Pallas kernels, body(): pl.pallas_call(kernel, out_shape=pltpu.VMEM((3, NODE_DEV + LANES), F32),...  48.6 us

profile of v8, /device:TPU:1, one launch (start us, length us, event | category | flops | bytes accessed | tf_op | source)
XLA Modules:
  0.0 49.8 jit_solution(6883696121906447939)
XLA Ops:
  0.6 48.6 %vcycle.1.all_ref = f32[3,1152]{1,0:T(4,128)S(1)} custom-call(f32[3,1024]{1,0:T(4,128)} %bitcast.13, f32[3,1024]{1,0:T(4,128)} %bitcast.14, s32[27,1024]{1,0:T(8,128)} %bitcast.12, f32[3,3,27,1024]{3,2,1,0:T(8,128)} %bitcast.10, s32[8,128]{1,0:T(8,128)} %bitcast.15, s32[1,32]{1,0:T(1,128)} %bitcast.17, f32[3,32]{1,0:T(4,128)} %bitcast.16, s32[32,27]{1,0:T(8,128)} %cq_h.1, ...), custom_call_target="tpu_custom_call" | custom-call | tf_op jit(solution)/shard_map/vcycle/pallas_call | solution.py:525
  49.2 0.6 %split.1 = (f32[3,1024]{1,0:T(4,128)}, f32[3,32]{1,0:T(4,128)}) custom-call(f32[3,1152]{1,0:T(4,128)S(1)} %vcycle.1.all_ref), custom_call_target="tpu_custom_call" | custom-call | tf_op jit(solution)/shard_map/split/pallas_call | solution.py:587
